TPU v7x, 32 devices: a whole 2x2x4 slice. The times are simulated.
32 devices in a mesh: prow: 4 (over x, core), pcol: 8 (over z, y).
Axes of the slice: x: 2, y: 2, z: 4, core: 2. Of those that a mesh axis runs over, the one named last changes fastest.
Arguments:
- matrix: float32 [4, 8, 768, 384], P('prow', 'pcol'), may hold values from -6 to 6
- pivots: int32 [3, 384], replicated, may hold values from 0 to 3071, as said below
- lower_inv: float32 [3, 384, 384], replicated, may hold values from -0.3125 to 0.3125
- upper_inv: float32 [3, 384, 384], replicated, may hold values from -0.015625 to 0.015625
Outputs:
- factored: float32 [4, 8, 768, 384], P('prow', 'pcol')
Inputs may be any that keep to these rules, and one draw needn't show every extreme that they name: Within one step s the indices pivots[s, i] are distinct, and each equals s * 384 + i or lies between (s + 1) * 384 and 3071.
All inputs are finite; a program needn't handle non-finite values.
Results may differ from a plain program's by a relative error of at most 0.0002.
Values sent between devices are 32-bit elements; how exact they have to be, the bound alone decides.
A program may use at most 64 MiB of HBM per device.

v0:
```python
import functools

import jax
import jax.numpy as jnp
from jax import lax
from jax.experimental import pallas as pl
from jax.experimental.pallas import tpu as pltpu
from jax.sharding import PartitionSpec as P

PRECISE = lax.Precision.HIGHEST
MESH = pl.DeviceIdType.MESH
CORES = 2


def grid_width(count):
    width = 1
    while (2 * width) * (2 * width) <= count:
        width *= 2
    return width if count % width == 0 else 1


def both(*conds):
    out = conds[0]
    for cond in conds[1:]:
        out = jnp.logical_and(out, cond)
    return out


def entry_barrier(neighbours):
    barrier = pltpu.get_barrier_semaphore()
    total = jnp.int32(0)
    for cond, device in neighbours:
        total = total + jnp.where(cond, 1, 0).astype(jnp.int32)

        @pl.when(cond)
        def _(device=device):
            pl.semaphore_signal(barrier, inc=1, device_id=device, device_id_type=MESH)

    pl.semaphore_wait(barrier, total)


def line_ways(prow, prow_count):
    x, core = prow // CORES, prow % CORES
    chips = prow_count // CORES
    return [
        (x + 1 < chips, {"prow": prow + CORES}),
        (x > 0, {"prow": prow - CORES}),
        (prow >= 0, {"prow": x * CORES + (CORES - 1 - core)}),
    ]


def line_sends(prow, prow_count, source):
    x, core = prow // CORES, prow % CORES
    ways = line_ways(prow, prow_count)
    sx, sc = source // CORES, source % CORES
    return [
        (both(ways[0][0], core == sc, x >= sx), ways[0][1]),
        (both(ways[1][0], core == sc, x <= sx), ways[1][1]),
        (core == sc, ways[2][1]),
    ]


def grid_ways(pcol, pcol_count):
    width = grid_width(pcol_count)
    height = pcol_count // width
    z, y = pcol // width, pcol % width
    return [
        (z + 1 < height, {"pcol": pcol + width}),
        (z > 0, {"pcol": pcol - width}),
        (y + 1 < width, {"pcol": pcol + 1}),
        (y > 0, {"pcol": pcol - 1}),
    ]


def tree_sends(pcol, pcol_count, source, first_axis):
    width = grid_width(pcol_count)
    height = pcol_count // width
    ways = grid_ways(pcol, pcol_count)
    pos = (pcol // width, pcol % width)
    src = (source // width, source % width)
    extent = (height, width)
    a, b = first_axis, 1 - first_axis
    away = {0: ways[0:2], 1: ways[2:4]}
    near = src[a] + 1 if src[a] + 1 < extent[a] else src[a] - 1
    trunk = pos[b] == src[b]
    off_row = pos[a] != src[a]
    sends = {}
    if extent[a] == 1:
        sends[a] = [pos[a] < 0, pos[a] < 0]
        sends[b] = [pos[b] >= src[b], pos[b] <= src[b]]
    else:
        back_up = both(pos[a] == near, jnp.logical_not(trunk))
        up = both(trunk, pos[a] >= src[a])
        down = both(trunk, pos[a] <= src[a])
        if near > src[a]:
            down = jnp.logical_or(down, back_up)
        else:
            up = jnp.logical_or(up, back_up)
        sends[a] = [up, down]
        sends[b] = [both(off_row, pos[b] >= src[b]), both(off_row, pos[b] <= src[b])]
    out = []
    for axis in (0, 1):
        for way in (0, 1):
            out.append((both(away[axis][way][0], sends[axis][way]), away[axis][way][1]))
    return out


class Flow:
    def __init__(self, mine, start_ref, land_ref, sends, send_sem, recv_sem, rows):
        self.mine, self.start_ref, self.land_ref = mine, start_ref, land_ref
        self.sends, self.send_sem, self.recv_sem, self.rows = sends, send_sem, recv_sem, rows

    def copy(self, chunk, way, ref):
        piece = pl.ds(chunk * self.rows, self.rows)
        return pltpu.make_async_remote_copy(
            src_ref=ref.at[piece],
            dst_ref=self.land_ref.at[piece],
            send_sem=self.send_sem.at[way, chunk],
            recv_sem=self.recv_sem.at[chunk],
            device_id=self.sends[way][1],
            device_id_type=MESH,
        )

    def send(self, chunk, ref):
        for way, (cond, _device) in enumerate(self.sends):

            @pl.when(cond)
            def _(way=way):
                self.copy(chunk, way, ref).start()

    def begin(self, chunk):
        @pl.when(self.mine)
        def _():
            self.send(chunk, self.start_ref)

    def relays(self):
        some = self.sends[0][0]
        for cond, _device in self.sends[1:]:
            some = jnp.logical_or(some, cond)
        return some

    def relay(self, chunk):
        @pl.when(jnp.logical_and(jnp.logical_not(self.mine), self.relays()))
        def _():
            self.copy(chunk, 0, self.land_ref).wait_recv()
            self.send(chunk, self.land_ref)

    def land(self, chunk):
        @pl.when(jnp.logical_not(jnp.logical_or(self.mine, self.relays())))
        def _():
            self.copy(chunk, 0, self.land_ref).wait_recv()

    def finish(self, chunk):
        for way, (cond, _device) in enumerate(self.sends):

            @pl.when(cond)
            def _(way=way):
                self.copy(chunk, way, self.land_ref).wait_send()


def gather_kernel(prow_count, chunks, tile_ref, strip_ref, send_sem, recv_sem, local_sem):
    prow = lax.axis_index("prow")
    entry_barrier(line_ways(prow, prow_count))
    rows = tile_ref.shape[0]
    own = pltpu.make_async_copy(tile_ref, strip_ref.at[prow], local_sem)
    own.start()
    flows = [
        Flow(
            prow == source,
            tile_ref,
            strip_ref.at[source],
            line_sends(prow, prow_count, source),
            send_sem.at[source],
            recv_sem.at[source],
            rows // chunks,
        )
        for source in range(prow_count)
    ]
    for chunk in range(chunks):
        for flow in flows:

            @pl.when(flow.mine)
            def _(flow=flow):
                for way, (cond, _device) in enumerate(flow.sends):

                    @pl.when(cond)
                    def _(way=way):
                        flow.copy(chunk, way, flow.start_ref).start()

    for chunk in range(chunks):
        for flow in flows:

            @pl.when(jnp.logical_not(flow.mine))
            def _(flow=flow):
                flow.copy(chunk, 0, flow.land_ref).wait_recv()
                for way, (cond, _device) in enumerate(flow.sends):

                    @pl.when(cond)
                    def _(way=way):
                        flow.copy(chunk, way, flow.land_ref).start()

    for chunk in range(chunks):
        for flow in flows:
            flow.finish(chunk)
    own.wait()


def gather_rows(tile, chunks):
    prow_count = lax.axis_size("prow")
    return pl.pallas_call(
        functools.partial(gather_kernel, prow_count, chunks),
        out_shape=jax.ShapeDtypeStruct((prow_count,) + tile.shape, tile.dtype),
        in_specs=[pl.BlockSpec(memory_space=pltpu.VMEM)],
        out_specs=pl.BlockSpec(memory_space=pltpu.VMEM),
        scratch_shapes=[
            pltpu.SemaphoreType.DMA((prow_count, 3, chunks)),
            pltpu.SemaphoreType.DMA((prow_count, chunks)),
            pltpu.SemaphoreType.DMA,
        ],
        compiler_params=pltpu.CompilerParams(collective_id=0, has_side_effects=True),
    )(tile)


def panel_kernel(
    prow_count, pcol_count, owner_row, owner_col, chunks, upper_chunks,
    lower_in, upper_in, lower_ref, upper_ref,
    send_sem, recv_sem, upper_send, upper_recv, local_sem,
):
    prow = lax.axis_index("prow")
    pcol = lax.axis_index("pcol")
    entry_barrier(line_ways(prow, prow_count) + grid_ways(pcol, pcol_count))
    half = lower_in.shape[0] // 2
    keep_lower = pltpu.make_async_copy(lower_in, lower_ref, local_sem.at[0])
    keep_upper = pltpu.make_async_copy(upper_in, upper_ref, local_sem.at[1])

    @pl.when(pcol == owner_col)
    def _():
        keep_lower.start()

    @pl.when(prow == owner_row)
    def _():
        keep_upper.start()

    flows = [
        Flow(
            pcol == owner_col,
            lower_in.at[pl.ds(part * half, half)],
            lower_ref.at[pl.ds(part * half, half)],
            tree_sends(pcol, pcol_count, owner_col, part),
            send_sem.at[part],
            recv_sem.at[part],
            half // chunks,
        )
        for part in range(2)
    ]
    upper = Flow(
        prow == owner_row, upper_in, upper_ref, line_sends(prow, prow_count, owner_row),
        upper_send, upper_recv, upper_in.shape[0] // upper_chunks,
    )
    for chunk in range(chunks):
        for flow in flows:
            flow.begin(chunk)
        if chunk < upper_chunks:
            upper.begin(chunk)
    for chunk in range(chunks):
        for flow in flows:
            flow.relay(chunk)
        if chunk < upper_chunks:
            upper.relay(chunk)
    for chunk in range(chunks):
        for flow in flows:
            flow.land(chunk)
            flow.finish(chunk)
        if chunk < upper_chunks:
            upper.land(chunk)
            upper.finish(chunk)

    @pl.when(pcol == owner_col)
    def _():
        keep_lower.wait()

    @pl.when(prow == owner_row)
    def _():
        keep_upper.wait()


def spread_panels(lower, upper, section, owner_row, owner_col, chunks, upper_chunks):
    prow_count = lax.axis_size("prow")
    pcol_count = lax.axis_size("pcol")
    return pl.pallas_call(
        functools.partial(
            panel_kernel, prow_count, pcol_count, owner_row, owner_col, chunks, upper_chunks
        ),
        out_shape=[
            jax.ShapeDtypeStruct(lower.shape, lower.dtype),
            jax.ShapeDtypeStruct(upper.shape, upper.dtype),
        ],
        in_specs=[pl.BlockSpec(memory_space=pltpu.VMEM)] * 2,
        out_specs=[pl.BlockSpec(memory_space=pltpu.VMEM)] * 2,
        scratch_shapes=[
            pltpu.SemaphoreType.DMA((2, 4, chunks)),
            pltpu.SemaphoreType.DMA((2, chunks)),
            pltpu.SemaphoreType.DMA((3, upper_chunks)),
            pltpu.SemaphoreType.DMA((upper_chunks,)),
            pltpu.SemaphoreType.DMA((2,)),
        ],
        compiler_params=pltpu.CompilerParams(collective_id=1 + section, has_side_effects=True),
    )(lower, upper)


def before_step(rows, pivot_list, start):
    width = pivot_list.shape[0]
    block = start + jnp.arange(width, dtype=jnp.int32)
    here = rows[:, None]
    moved_in = jnp.where(here == block[None, :], pivot_list[None, :] - here, 0)
    moved_out = jnp.where(
        (here == pivot_list[None, :]) & (pivot_list != block)[None, :], block[None, :] - here, 0
    )
    return rows + jnp.sum(moved_in + moved_out, axis=1, dtype=jnp.int32)


def on_device(matrix, pivots, lower_inv, upper_inv):
    prow_count = lax.axis_size("prow")
    pcol_count = lax.axis_size("pcol")
    prow_index = lax.axis_index("prow")
    pcol_index = lax.axis_index("pcol")
    tile = matrix[0, 0]
    local_rows, local_cols = tile.shape
    width = lower_inv.shape[1]
    sections = pivots.shape[0]
    row_ids = jnp.arange(local_rows, dtype=jnp.int32)
    global_rows = (row_ids // width * prow_count + prow_index) * width + row_ids % width
    col_ids = jnp.arange(local_cols, dtype=jnp.int32)
    global_cols = (col_ids // width * pcol_count + pcol_index) * width + col_ids % width

    origin = global_rows
    for section in reversed(range(sections)):
        origin = before_step(origin, pivots[section], section * width)
    block = origin // width
    place = block % prow_count * local_rows + block // prow_count * width + origin % width
    strip = gather_rows(tile, 4).reshape(prow_count * local_rows, local_cols)
    tile = strip.at[place].get(mode="promise_in_bounds")

    for section in range(sections):
        finish = (section + 1) * width
        owner_row = section % prow_count
        owner_col = section % pcol_count
        row_start = section // prow_count * width
        col_start = section // pcol_count * width
        lower_unit = jnp.eye(width, dtype=jnp.float32) + jnp.tril(lower_inv[section], -1)
        upper_tri = jnp.triu(upper_inv[section])
        col_mask = (global_cols >= finish)[None, :]
        row_mask = (global_rows >= finish)[:, None]
        current = tile[row_start : row_start + width]
        panel = tile[:, col_start : col_start + width]
        upper = jnp.where(
            col_mask,
            jnp.dot(lower_unit, current, precision=PRECISE, preferred_element_type=jnp.float32),
            0.0,
        )
        lower = jnp.where(
            row_mask,
            jnp.dot(panel, upper_tri, precision=PRECISE, preferred_element_type=jnp.float32),
            0.0,
        )
        lower, upper = spread_panels(lower, upper, section, owner_row, owner_col, 8, 4)
        stored = jnp.where(col_mask & (prow_index == owner_row), upper, current)
        base = tile.at[row_start : row_start + width].set(stored)
        kept = jnp.where(
            row_mask & (pcol_index == owner_col), lower, base[:, col_start : col_start + width]
        )
        base = base.at[:, col_start : col_start + width].set(kept)
        tile = base - jnp.dot(
            lower, upper, precision=PRECISE, preferred_element_type=jnp.float32
        )
    return tile[None, None]


def solution(mesh):
    return jax.shard_map(
        on_device,
        mesh=mesh,
        in_specs=(P("prow", "pcol", None, None), P(), P(), P()),
        out_specs=P("prow", "pcol", None, None),
        check_vma=False,
    )
```

profile of v0, /device:TPU:26, one launch (start us, length us, event | category | flops | bytes accessed | tf_op | source)
XLA Modules:
  0.0 161.5 jit_solution(2767665337818178120)
XLA Ops:
  0.0 0.8 slice_reduce_fusion.1
  0.8 0.8 compare_reduce_fusion
  1.7 0.6 add_reduce_fusion.2
  2.3 0.6 add_reduce_fusion.1
  2.8 0.6 add_reduce_fusion
  3.4 0.1 fusion.36
  3.5 34.7 %shard_map.61 = f32[4,768,384]{2,1,0:T(8,128)} custom-call(f32[768,384]{1,0:T(8,128)} %bitcast.38), custom_call_target="tpu_custom_call" | custom-call | tf_op jit(solution)/shard_map/pallas_call | solution.py:210
  38.2 4.8 %gather_fusion = f32[768,384]{1,0:T(8,128)S(1)} fusion(f32[3072,384]{1,0:T(8,128)} %bitcast.37, s32[1024]{0:T(1024)S(1)} %pad_clamp_fusion), kind=kCustom, calls=%fused_computation | custom fusion | bytes 2362368 | tf_op jit(solution)/shard_map/gather | solution.py:342
  43.1 4.5 %convolution_select_fusion.2.lower_in = f32[768,384]{1,0:T(8,128)} fusion(f32[768,384]{1,0:T(8,128)S(1)} %gather_fusion, f32[3,384,384]{2,1,0:T(8,128)} %param.25, pred[768]{0:T(1024)(128)(4,1)S(1)} %get-tuple-element.121, s32[384]{0:T(512)S(1)} %iota_add_fusion), kind=kOutput, calls=%fused_computation.6 | convolution fusion | flops 1359544320 | bytes 2951424 | tf_op jit(solution)/shard_map/dot_general | solution.py:363
  47.6 3.2 %convolution_select_fusion.5.upper_in = f32[384,384]{1,0:T(8,128)} fusion(f32[3,384,384]{2,1,0:T(8,128)} %param.24, f32[768,384]{1,0:T(8,128)S(1)} %gather_fusion, s32[384]{0:T(512)S(1)} %iota_add_fusion, pred[384]{0:T(512)(128)(4,1)S(1)} %get-tuple-element.126), kind=kOutput, calls=%fused_computation.10 | convolution fusion | flops 680361984 | bytes 1772032 | tf_op jit(solution)/shard_map/dot_general | solution.py:358
  50.8 31.8 %shard_map.62 = (f32[768,384]{1,0:T(8,128)}, f32[384,384]{1,0:T(8,128)}) custom-call(f32[768,384]{1,0:T(8,128)} %convolution_select_fusion.2.lower_in, f32[384,384]{1,0:T(8,128)} %convolution_select_fusion.5.upper_in), custom_call_target="tpu_custom_call" | custom-call | tf_op jit(solution)/shard_map/pallas_call | solution.py:290
  82.6 0.0 copy-start.1
  82.6 0.0 copy-start.3
  82.6 1.3 select_dynamic-update-slice_fusion.2
  83.9 0.0 copy-done.1
  83.9 0.3 copy-done.3
  84.2 2.4 %convolution_subtract_fusion.2 = f32[768,384]{1,0:T(8,128)S(1)} fusion(f32[768,384]{1,0:T(8,128)S(1)} %copy-done.3, f32[384,384]{1,0:T(8,128)S(1)} %copy-done.1, f32[768,384]{1,0:T(8,128)S(1)} %select_dynamic-update-slice_fusion.2, pred[768]{0:T(1024)(128)(4,1)S(1)} %get-tuple-element.122), kind=kOutput, calls=%fused_computation.3 | convolution fusion | flops 1359544320 | bytes 4129536 | tf_op jit(solution)/shard_map/dot_general | solution.py:373
  86.6 4.5 %convolution_select_fusion.1.lower_in = f32[768,384]{1,0:T(8,128)} fusion(f32[768,384]{1,0:T(8,128)S(1)} %convolution_subtract_fusion.2, f32[3,384,384]{2,1,0:T(8,128)} %param.25, pred[768]{0:T(1024)(128)(4,1)S(1)} %get-tuple-element.119, s32[384]{0:T(512)S(1)} %iota_add_fusion), kind=kOutput, calls=%fused_computation.5 | convolution fusion | flops 1359544320 | bytes 2951424 | tf_op jit(solution)/shard_map/dot_general | solution.py:363
  91.2 3.2 %convolution_select_fusion.4.upper_in = f32[384,384]{1,0:T(8,128)} fusion(f32[3,384,384]{2,1,0:T(8,128)} %param.24, f32[768,384]{1,0:T(8,128)S(1)} %convolution_subtract_fusion.2, s32[384]{0:T(512)S(1)} %iota_add_fusion, pred[384]{0:T(512)(128)(4,1)S(1)} %get-tuple-element.127), kind=kOutput, calls=%fused_computation.9 | convolution fusion | flops 680361984 | bytes 1772032 | tf_op jit(solution)/shard_map/dot_general | solution.py:358
  94.4 24.7 %shard_map.63 = (f32[768,384]{1,0:T(8,128)}, f32[384,384]{1,0:T(8,128)}) custom-call(f32[768,384]{1,0:T(8,128)} %convolution_select_fusion.1.lower_in, f32[384,384]{1,0:T(8,128)} %convolution_select_fusion.4.upper_in), custom_call_target="tpu_custom_call" | custom-call | tf_op jit(solution)/shard_map/pallas_call | solution.py:290
  119.1 0.0 copy-start
  119.1 1.2 select_dynamic-update-slice_fusion.1
  120.3 0.0 copy-done
  120.4 4.0 %convolution_subtract_fusion.1 = f32[768,384]{1,0:T(8,128)S(1)} fusion(f32[768,384]{1,0:T(8,128)} %get-tuple-element.109, f32[384,384]{1,0:T(8,128)S(1)} %copy-done, f32[768,384]{1,0:T(8,128)S(1)} %select_dynamic-update-slice_fusion.1, pred[768]{0:T(1024)(128)(4,1)S(1)} %get-tuple-element.123), kind=kOutput, calls=%fused_computation.2 | convolution fusion | flops 1359544320 | bytes 4129536 | tf_op jit(solution)/shard_map/dot_general | solution.py:373
  124.3 4.5 %convolution_select_fusion.lower_in = f32[768,384]{1,0:T(8,128)} fusion(f32[768,384]{1,0:T(8,128)S(1)} %convolution_subtract_fusion.1, f32[3,384,384]{2,1,0:T(8,128)} %param.25, pred[768]{0:T(1024)(128)(4,1)S(1)} %get-tuple-element.120, s32[384]{0:T(512)S(1)} %iota_add_fusion), kind=kOutput, calls=%fused_computation.4 | convolution fusion | flops 1359544320 | bytes 2951424 | tf_op jit(solution)/shard_map/dot_general | solution.py:363
  128.8 3.2 %convolution_select_fusion.3.upper_in = f32[384,384]{1,0:T(8,128)} fusion(f32[3,384,384]{2,1,0:T(8,128)} %param.24, f32[768,384]{1,0:T(8,128)S(1)} %convolution_subtract_fusion.1, s32[384]{0:T(512)S(1)} %iota_add_fusion, pred[384]{0:T(512)(128)(4,1)S(1)} %get-tuple-element.125), kind=kOutput, calls=%fused_computation.8 | convolution fusion | flops 680361984 | bytes 1772032 | tf_op jit(solution)/shard_map/dot_general | solution.py:358
  132.1 24.4 %shard_map.64 = (f32[768,384]{1,0:T(8,128)}, f32[384,384]{1,0:T(8,128)}) custom-call(f32[768,384]{1,0:T(8,128)} %convolution_select_fusion.lower_in, f32[384,384]{1,0:T(8,128)} %convolution_select_fusion.3.upper_in), custom_call_target="tpu_custom_call" | custom-call | tf_op jit(solution)/shard_map/pallas_call | solution.py:290
  156.5 0.0 copy-start.2
  156.5 0.0 copy-start.4
  156.5 1.3 select_dynamic-update-slice_fusion
  157.8 0.0 copy-done.2
  157.8 0.3 copy-done.4
  158.1 3.4 %fusion = f32[1,1,768,384]{3,2,1,0:T(8,128)} fusion(f32[768,384]{1,0:T(8,128)S(1)} %copy-done.4, f32[384,384]{1,0:T(8,128)S(1)} %copy-done.2, f32[768,384]{1,0:T(8,128)S(1)} %select_dynamic-update-slice_fusion, pred[768]{0:T(1024)(128)(4,1)S(1)} %get-tuple-element.124), kind=kOutput, calls=%fused_computation.7 | convolution fusion | flops 1359544320 | bytes 4129536 | tf_op jit(solution)/shard_map/dot_general | solution.py:373
  (13 shorter events, 0.2 us)
Async XLA Ops:
  82.6 1.3 copy-start.1
  82.6 1.6 %copy-start.3 = (f32[768,384]{1,0:T(8,128)S(1)}, f32[768,384]{1,0:T(8,128)}, u32[]{:S(2)}) copy-start(f32[768,384]{1,0:T(8,128)} %get-tuple-element.107) | copy-start | bytes 3538948
  119.1 1.3 copy-start
  156.5 1.3 copy-start.2
  156.5 1.6 %copy-start.4 = (f32[768,384]{1,0:T(8,128)S(1)}, f32[768,384]{1,0:T(8,128)}, u32[]{:S(2)}) copy-start(f32[768,384]{1,0:T(8,128)} %get-tuple-element.111) | copy-start | bytes 3538948
where the time goes:
time: 164 us; the launch traced here: 162 us
  Pallas kernels  115 us (70%)
  matrix products  33 us (20%)
  other arithmetic  6.61 us (4%)
  local copies, waits for them, and re-layouts  6.23 us (4%)
    pallas_call x3, Pallas kernels, spread_panels(): pl.pallas_call(functools.partial(panel_kernel, prow_count, pcol_count, ow...  80.8 us
    pallas_call x1, Pallas kernels, gather_rows(): pl.pallas_call(functools.partial(gather_kernel, prow_count, chunks), out_...  34.7 us
    dot_general x3, matrix products, on_device(): jnp.dot(panel, upper_tri, precision=PRECISE, preferred_element_type=jnp.f...  13.5 us
    dot_general x3, matrix products, on_device(): jnp.dot(lower, upper, precision=PRECISE, preferred_element_type=jnp.float32)  9.73 us
    dot_general x3, matrix products, on_device(): jnp.dot(lower_unit, current, precision=PRECISE, preferred_element_type=jn...  9.72 us
    gather x1, local copies, waits for them, and re-layouts, on_device(): tile = strip.at[place].get(mode='promise_in_bounds')  4.8 us
    scatter x3, other arithmetic, on_device(): base = tile.at[row_start:row_start + width].set(stored)  3.83 us

commit v1 on v0

v1 whole, which is shorter than its diff:
```python
import functools

import jax
import jax.numpy as jnp
from jax import lax
from jax.experimental import pallas as pl
from jax.experimental.pallas import tpu as pltpu
from jax.sharding import PartitionSpec as P

MESH = pl.DeviceIdType.MESH
CORES = 2
F32 = jnp.float32
BF16 = jnp.bfloat16
HOP = 2


def grid_width(count):
    width = 1
    while (2 * width) * (2 * width) <= count:
        width *= 2
    return width if count % width == 0 else 1


def both(*conds):
    out = conds[0]
    for cond in conds[1:]:
        out = jnp.logical_and(out, cond)
    return out


def entry_barrier(neighbours):
    barrier = pltpu.get_barrier_semaphore()
    total = jnp.int32(0)
    for cond, device in neighbours:
        total = total + jnp.where(cond, 1, 0).astype(jnp.int32)

        @pl.when(cond)
        def _(device=device):
            pl.semaphore_signal(barrier, inc=1, device_id=device, device_id_type=MESH)

    pl.semaphore_wait(barrier, total)


def line_ways(prow, prow_count):
    x, core = prow // CORES, prow % CORES
    chips = prow_count // CORES
    return [
        (x + 1 < chips, {"prow": prow + CORES}),
        (x > 0, {"prow": prow - CORES}),
        (prow >= 0, {"prow": x * CORES + (CORES - 1 - core)}),
    ]


def line_sends(prow, prow_count, source):
    x, core = prow // CORES, prow % CORES
    ways = line_ways(prow, prow_count)
    sx, sc = source // CORES, source % CORES
    return [
        (both(ways[0][0], core == sc, x >= sx), ways[0][1]),
        (both(ways[1][0], core == sc, x <= sx), ways[1][1]),
        (core == sc, ways[2][1]),
    ]


def grid_ways(pcol, pcol_count):
    width = grid_width(pcol_count)
    height = pcol_count // width
    z, y = pcol // width, pcol % width
    return [
        (z + 1 < height, {"pcol": pcol + width}),
        (z > 0, {"pcol": pcol - width}),
        (y + 1 < width, {"pcol": pcol + 1}),
        (y > 0, {"pcol": pcol - 1}),
    ]


def tree_sends(pcol, pcol_count, source, first_axis):
    width = grid_width(pcol_count)
    height = pcol_count // width
    ways = grid_ways(pcol, pcol_count)
    pos = (pcol // width, pcol % width)
    src = (source // width, source % width)
    extent = (height, width)
    a, b = first_axis, 1 - first_axis
    away = {0: ways[0:2], 1: ways[2:4]}
    near = src[a] + 1 if src[a] + 1 < extent[a] else src[a] - 1
    trunk = pos[b] == src[b]
    off_row = pos[a] != src[a]
    sends = {}
    if extent[a] == 1:
        sends[a] = [pos[a] < 0, pos[a] < 0]
        sends[b] = [pos[b] >= src[b], pos[b] <= src[b]]
    else:
        back_up = both(pos[a] == near, jnp.logical_not(trunk))
        up = both(trunk, pos[a] >= src[a])
        down = both(trunk, pos[a] <= src[a])
        if near > src[a]:
            down = jnp.logical_or(down, back_up)
        else:
            up = jnp.logical_or(up, back_up)
        sends[a] = [up, down]
        sends[b] = [both(off_row, pos[b] >= src[b]), both(off_row, pos[b] <= src[b])]
    out = []
    for axis in (0, 1):
        for way in (0, 1):
            out.append((both(away[axis][way][0], sends[axis][way]), away[axis][way][1]))
    return out


def tree_hops(pcol, pcol_count, source, first_axis):
    width = grid_width(pcol_count)
    extent = (pcol_count // width, width)
    pos = (pcol // width, pcol % width)
    src = (source // width, source % width)
    a, b = first_axis, 1 - first_axis
    straight = jnp.abs(pos[a] - src[a]) + jnp.abs(pos[b] - src[b])
    if extent[a] == 1:
        return straight
    return straight + jnp.where(both(pos[a] == src[a], pos[b] != src[b]), 2, 0)


class Flow:
    def __init__(self, mine, start_ref, land_ref, sends, send_sem, recv_sem, rows):
        self.mine, self.start_ref, self.land_ref = mine, start_ref, land_ref
        self.sends, self.send_sem, self.recv_sem, self.rows = sends, send_sem, recv_sem, rows

    def copy(self, chunk, way, ref):
        piece = pl.ds(chunk * self.rows, self.rows)
        return pltpu.make_async_remote_copy(
            src_ref=ref.at[piece],
            dst_ref=self.land_ref.at[piece],
            send_sem=self.send_sem.at[way, chunk],
            recv_sem=self.recv_sem.at[chunk],
            device_id=self.sends[way][1],
            device_id_type=MESH,
        )

    def send(self, chunk, ref):
        for way, (cond, _device) in enumerate(self.sends):

            @pl.when(cond)
            def _(way=way):
                self.copy(chunk, way, ref).start()

    def pass_on(self, chunk):
        @pl.when(jnp.logical_not(self.mine))
        def _():
            self.copy(chunk, 0, self.land_ref).wait_recv()
            self.send(chunk, self.land_ref)

    def finish(self, chunk):
        for way, (cond, _device) in enumerate(self.sends):

            @pl.when(cond)
            def _(way=way):
                self.copy(chunk, way, self.land_ref).wait_send()


def split2(value):
    high = value.astype(BF16)
    low = (value - high.astype(F32)).astype(BF16)
    return high, low


def split3(value):
    high = value.astype(BF16)
    rest = value - high.astype(F32)
    middle = rest.astype(BF16)
    low = (rest - middle.astype(F32)).astype(BF16)
    return high, middle, low


def wide(value):
    high, low = split2(value)
    return jnp.concatenate([high, high, low], axis=1)


def dot(left, right):
    return jnp.dot(left, right, preferred_element_type=F32)


def factor_kernel(
    prow_count, pcol_count, sections, width, blocks,
    tile_ref, pivots_ref, lower_ref, upper_ref, out_ref,
    first, pivot, low_in, up_in, parts, top, top_parts, picked, picked_in,
    row_panel, col_panel, row_stack, low_wide, up_stack, core_stack,
    local_sem, top_send, top_recv, pick_send, pick_recv,
    row_send, row_recv, col_send, col_recv,
):
    prow = lax.axis_index("prow")
    pcol = lax.axis_index("pcol")
    x, core = prow // CORES, prow % CORES
    chips = prow_count // CORES
    step_rows = width // 3
    tiles = width // step_rows
    relay_rows = col_panel.shape[1] // (2 * col_recv.shape[2])
    span = 2 * relay_rows
    per_block = width // span

    load_tile = pltpu.make_async_copy(tile_ref, first, local_sem.at[0])
    load_pivots = pltpu.make_async_copy(pivots_ref, pivot, local_sem.at[1])
    load_pivots.start()
    load_tile.start()
    owns_row = prow < sections
    owns_col = pcol < sections

    @pl.when(owns_row)
    def _():
        pltpu.make_async_copy(lower_ref.at[prow], low_in, local_sem.at[2]).start()

    @pl.when(owns_col)
    def _():
        pltpu.make_async_copy(upper_ref.at[pcol], up_in, local_sem.at[3]).start()

    top_flows = [
        Flow(
            prow == s, tile_ref, top.at[pl.ds(s * width, width)],
            line_sends(prow, prow_count, s), top_send.at[s], top_recv.at[s], step_rows,
        )
        for s in range(sections)
    ]
    row_flows = [
        Flow(
            prow == s, row_panel.at[s], row_panel.at[s],
            line_sends(prow, prow_count, s), row_send.at[s], row_recv.at[s], step_rows,
        )
        for s in range(sections)
    ]

    entry_barrier(line_ways(prow, prow_count) + grid_ways(pcol, pcol_count))

    for s in range(sections):

        @pl.when(prow == s)
        def _(s=s):
            for chunk in range(tiles):
                top_flows[s].send(chunk, tile_ref)
            pltpu.make_async_copy(
                tile_ref.at[pl.ds(0, width)], top.at[pl.ds(s * width, width)], local_sem.at[4]
            ).start()

    def lanes(count):
        return lax.broadcasted_iota(jnp.int32, (1, count), 1).astype(F32)

    def column(start):
        ids = lax.broadcasted_iota(jnp.int32, (step_rows, 1), 0)
        return (ids + start).astype(F32)

    def pivot_row(s):
        return pivot[pl.ds(s, 1), :].astype(F32)

    def undo(rows, upto):
        for s in reversed(range(upto)):
            listed = pivot_row(s)
            shift = lanes(width) + F32(s * width) - listed
            moved = jnp.where(rows == listed, shift, F32(0))
            rows = rows + jnp.sum(moved, axis=1, keepdims=True)
        return rows

    def one_hot(rows, ids):
        return jnp.where(rows == ids, F32(1), F32(0)).astype(BF16)

    load_pivots.wait()
    load_tile.wait()

    def cut_tile(i, carry):
        at = pl.ds(pl.multiple_of(i * step_rows, step_rows), step_rows)
        for k, part in enumerate(split3(first[at, :])):
            parts[k, at, :] = part
        return carry

    lax.fori_loop(0, tiles * blocks, cut_tile, 0)

    def pick_copy(s, slot, where, device):
        return pltpu.make_async_remote_copy(
            src_ref=picked.at[s],
            dst_ref=picked_in.at[s, slot],
            send_sem=pick_send.at[s, where],
            recv_sem=pick_recv.at[s, slot],
            device_id=device,
            device_id_type=MESH,
        )

    partner = {"prow": x * CORES + (CORES - 1 - core)}
    held_ids = jnp.concatenate(
        [
            lanes(width) + ((block * prow_count + prow) * width).astype(F32)
            for block in range(blocks)
        ],
        axis=1,
    )
    for s in range(sections):

        def pick(i, carry, s=s):
            start = i * step_rows
            at = pl.ds(pl.multiple_of(start, step_rows), step_rows)
            rows = jnp.sum(
                jnp.where(column(start) == lanes(width), pivot_row(s), F32(0)),
                axis=1, keepdims=True,
            )
            chosen = one_hot(undo(rows, s), held_ids)
            picked[s, at, :] = (
                dot(chosen, parts[2]) + dot(chosen, parts[1]) + dot(chosen, parts[0])
            )
            return carry

        lax.fori_loop(0, tiles, pick, 0)

        @pl.when(core != s % CORES)
        def _(s=s):
            pick_copy(s, 0, 0, partner).start()

    def add_in(s, slot):
        pick_copy(s, slot, 1, partner).wait_recv()

        def add(i, carry):
            at = pl.ds(pl.multiple_of(i * step_rows, step_rows), step_rows)
            picked[s, at, :] += picked_in[s, slot, at, :]
            return carry

        lax.fori_loop(0, tiles, add, 0)

    def pass_picked(s, when):
        owner = s // CORES

        @pl.when(both(core == s % CORES, x != owner, when))
        def _():
            add_in(s, 0)

            @pl.when(both(x < owner, x > 0))
            def _():
                add_in(s, 1)

            @pl.when(both(x > owner, x < chips - 1))
            def _():
                add_in(s, 2)

            @pl.when(x < owner)
            def _():
                pick_copy(s, 1, 1, {"prow": prow + CORES}).start()

            @pl.when(x > owner)
            def _():
                pick_copy(s, 2, 1, {"prow": prow - CORES}).start()

    def urgent(s):
        return pcol > 0 if s == 0 else pcol == 0

    for s in range(sections):
        pass_picked(s, urgent(s))

    @pl.when(owns_row)
    def _():
        pltpu.make_async_copy(lower_ref.at[prow], low_in, local_sem.at[2]).wait()

        def prepare(i, carry):
            start = i * step_rows
            at = pl.ds(pl.multiple_of(start, step_rows), step_rows)
            below = column(start) > lanes(width)
            same = column(start) == lanes(width)
            unit = jnp.where(below, low_in[at, :], jnp.where(same, F32(1), F32(0)))
            low_wide[at, :] = wide(unit)
            return carry

        lax.fori_loop(0, tiles, prepare, 0)

    def stack(ref, i, value):
        high, low = split2(value)
        start = i * step_rows
        for k, part in enumerate((high, low, high)):
            at = pl.ds(pl.multiple_of(k * width + start, step_rows), step_rows)
            ref[at, :] = part

    @pl.when(owns_col)
    def _():
        pltpu.make_async_copy(upper_ref.at[pcol], up_in, local_sem.at[3]).wait()

        def prepare(i, carry):
            start = i * step_rows
            at = pl.ds(pl.multiple_of(start, step_rows), step_rows)
            kept = jnp.where(column(start) <= lanes(width), up_in[at, :], F32(0))
            stack(up_stack, i, kept)
            return carry

        lax.fori_loop(0, tiles, prepare, 0)

    for chunk in range(tiles):
        for flow in top_flows:
            flow.pass_on(chunk)
    for s in range(sections):

        @pl.when(prow == s)
        def _(s=s):
            pltpu.make_async_copy(
                tile_ref.at[pl.ds(0, width)], top.at[pl.ds(s * width, width)], local_sem.at[4]
            ).wait()

    def take_picked(s):
        owner = s // CORES
        add_in(s, 0)
        if owner > 0:
            add_in(s, 1)
        if owner < chips - 1:
            add_in(s, 2)
        out_ref[pl.ds(0, width), :] = picked[s]

    def row_product(s):
        def cut(i, carry):
            at = pl.ds(pl.multiple_of(i * step_rows, step_rows), step_rows)
            stack(core_stack, i, out_ref[at, :])
            return carry

        lax.fori_loop(0, tiles, cut, 0)
        for chunk in range(tiles):
            at = pl.ds(chunk * step_rows, step_rows)
            value = dot(low_wide[at, :], core_stack[...])
            row_panel[s, at, :] = value
            out_ref[at, :] = value
            if chunk > 0:
                row_flows[s].send(chunk - 1, row_panel.at[s])
        row_flows[s].send(tiles - 1, row_panel.at[s])

    @pl.when(both(prow == 0, pcol > 0))
    def _():
        take_picked(0)
        row_product(0)

    for s in range(sections):
        pass_picked(s, jnp.logical_not(urgent(s)))

    def cut_top(i, carry):
        at = pl.ds(pl.multiple_of(i * step_rows, step_rows), step_rows)
        for k, part in enumerate(split3(top[at, :])):
            top_parts[k, at, :] = part
        return carry

    lax.fori_loop(0, tiles * sections, cut_top, 0)

    def settle(block):
        def place(i, carry):
            start = i * step_rows
            at = pl.ds(pl.multiple_of(block * width + start, step_rows), step_rows)
            rows = column(start + (block * prow_count + prow) * width)
            rows = undo(rows, sections)
            chosen = one_hot(rows, lanes(sections * width))
            value = (
                dot(chosen, top_parts[2]) + dot(chosen, top_parts[1]) + dot(chosen, top_parts[0])
            )
            out_ref[at, :] = jnp.where(rows < F32(sections * width), value, first[at, :])
            return carry

        lax.fori_loop(0, tiles, place, 0)

    for block in range(1, blocks):
        settle(block)

    @pl.when(jnp.logical_not(owns_row))
    def _():
        settle(0)

    sends = [
        [tree_sends(pcol, pcol_count, s, k) for k in range(2)] for s in range(sections)
    ]

    def live(s):
        return jnp.where(prow > s, blocks, blocks - 1)

    def place_of(s, i):
        turn = lax.div(i, per_block)
        block = blocks - 1 - turn if s == 0 else blocks - live(s) + turn
        return block * width + (i - turn * per_block) * span

    def col_copy(s, k, i, way):
        start = pl.multiple_of(place_of(s, i) + k * relay_rows, relay_rows)
        piece = pl.ds(start, relay_rows)
        return pltpu.make_async_remote_copy(
            src_ref=col_panel.at[s, piece],
            dst_ref=col_panel.at[s, piece],
            send_sem=col_send.at[s, k, way, i],
            recv_sem=col_recv.at[s, k, i],
            device_id=sends[s][k][way][1],
            device_id_type=MESH,
        )

    def col_start(s, k, i):
        for way in range(4):

            @pl.when(sends[s][k][way][0])
            def _(way=way):
                col_copy(s, k, i, way).start()

    def update(s, at):
        return out_ref[at, :] - dot(wide(col_panel[s, at, :]), row_stack[...])

    def produce(s, start, stop, updated):
        def body(i, carry):
            at = pl.ds(pl.multiple_of(place_of(s, i), span), span)
            value = update(s - 1, at) if updated else out_ref[at, :]
            value = dot(wide(value), up_stack[...])
            col_panel[s, at, :] = value
            out_ref[at, :] = value

            @pl.when(i > start)
            def _():
                for k in range(2):
                    col_start(s, k, i - 1)

            return carry

        lax.fori_loop(start, stop, body, 0)
        for k in range(2):
            col_start(s, k, stop - 1)

    def relay(s, hook):
        hops = [tree_hops(pcol, pcol_count, s, k) for k in range(2)]
        late = [HOP * jnp.maximum(hops[k] - hops[1 - k], 0) for k in range(2)]
        count = live(s) * per_block

        def body(t, carry):
            for k in range(2):
                i = t - late[k]

                @pl.when(both(i >= 0, i < count))
                def _(k=k, i=i):
                    col_copy(s, k, i, 0).wait_recv()
                    col_start(s, k, i)

            return carry

        lax.fori_loop(0, per_block, body, 0)
        hook()
        lax.fori_loop(per_block, count + late[0] + late[1], body, 0)

    def update_block(s, block):
        def body(i, carry):
            at = pl.ds(pl.multiple_of(block * width + i * step_rows, step_rows), step_rows)
            out_ref[at, :] = update(s, at)
            return carry

        lax.fori_loop(0, tiles, body, 0)

    @pl.when(pcol == 0)
    def _():
        produce(0, 0, (blocks - 1) * per_block, False)
        for s in range(sections):

            @pl.when(prow == s)
            def _(s=s):
                take_picked(s)

        @pl.when(prow > 0)
        def _():
            produce(0, (blocks - 1) * per_block, blocks * per_block, False)

    for s in range(sections):

        @pl.when(pcol != s)
        def _(s=s):
            def hook():
                @pl.when(pcol > s)
                def _():
                    for chunk in range(tiles):
                        row_flows[s].pass_on(chunk)

            relay(s, hook)

        @pl.when(pcol > s)
        def _(s=s):
            if s == 0:
                for other in range(1, sections):

                    @pl.when(prow == other)
                    def _(other=other):
                        take_picked(other)

            def cut(i, carry):
                at = pl.ds(pl.multiple_of(i * step_rows, step_rows), step_rows)
                stack(row_stack, i, row_panel[s, at, :])
                return carry

            lax.fori_loop(0, tiles, cut, 0)
            last = s + 1 == sections

            def plain():
                @pl.when(prow > s)
                def _():
                    update_block(s, 0)

                if not last:

                    @pl.when(prow == s + 1)
                    def _():
                        row_product(s + 1)

                for block in range(1, blocks):
                    update_block(s, block)

            if last:
                plain()
            else:
                pl.when(pcol > s + 1)(plain)

                @pl.when(pcol == s + 1)
                def _():
                    produce(s + 1, 0, live(s + 1) * per_block, True)

                    @pl.when(prow == s + 1)
                    def _():
                        update_block(s, 0)

    for s in range(sections):
        for chunk in range(tiles):
            top_flows[s].finish(chunk)

        @pl.when(pcol > s)
        def _(s=s):
            for chunk in range(tiles):
                row_flows[s].finish(chunk)

        owner = s // CORES

        @pl.when(core != s % CORES)
        def _(s=s):
            pick_copy(s, 0, 0, partner).wait_send()

        @pl.when(both(core == s % CORES, x != owner))
        def _(s=s):
            pick_copy(s, 0, 1, partner).wait_send()

        for k in range(2):
            for way in range(4):

                @pl.when(sends[s][k][way][0])
                def _(s=s, k=k, way=way):
                    def body(i, carry):
                        col_copy(s, k, i, way).wait_send()
                        return carry

                    lax.fori_loop(0, live(s) * per_block, body, 0)


def on_device(matrix, pivots, lower_inv, upper_inv):
    prow_count = lax.axis_size("prow")
    pcol_count = lax.axis_size("pcol")
    tile = matrix[0, 0]
    rows, width = tile.shape
    sections = pivots.shape[0]
    blocks = rows // width
    assert width == pivots.shape[1] and sections <= prow_count and sections <= pcol_count
    tiles = 3
    relays = blocks * 6
    dma = pltpu.SemaphoreType.DMA
    out = pl.pallas_call(
        functools.partial(factor_kernel, prow_count, pcol_count, sections, width, blocks),
        out_shape=jax.ShapeDtypeStruct(tile.shape, tile.dtype),
        in_specs=[pl.BlockSpec(memory_space=pl.ANY)] * 4,
        out_specs=pl.BlockSpec(memory_space=pltpu.VMEM),
        scratch_shapes=[
            pltpu.VMEM((rows, width), F32),
            pltpu.VMEM(pivots.shape, jnp.int32),
            pltpu.VMEM((width, width), F32),
            pltpu.VMEM((width, width), F32),
            pltpu.VMEM((3, rows, width), BF16),
            pltpu.VMEM((sections * width, width), F32),
            pltpu.VMEM((3, sections * width, width), BF16),
            pltpu.VMEM((sections, width, width), F32),
            pltpu.VMEM((sections, 3, width, width), F32),
            pltpu.VMEM((sections, width, width), F32),
            pltpu.VMEM((sections, rows, width), F32),
            pltpu.VMEM((3 * width, width), BF16),
            pltpu.VMEM((width, 3 * width), BF16),
            pltpu.VMEM((3 * width, width), BF16),
            pltpu.VMEM((3 * width, width), BF16),
            dma((5,)),
            dma((sections, 3, tiles)),
            dma((sections, tiles)),
            dma((sections, 2)),
            dma((sections, 3)),
            dma((sections, 3, tiles)),
            dma((sections, tiles)),
            dma((sections, 2, 4, relays)),
            dma((sections, 2, relays)),
        ],
        compiler_params=pltpu.CompilerParams(
            collective_id=0, has_side_effects=True, vmem_limit_bytes=60 * 1024 * 1024
        ),
    )(tile, pivots, lower_inv, upper_inv)
    return out[None, None]


def solution(mesh):
    return jax.shard_map(
        on_device,
        mesh=mesh,
        in_specs=(P("prow", "pcol", None, None), P(), P(), P()),
        out_specs=P("prow", "pcol", None, None),
        check_vma=False,
    )
```

time: 164 us -> 102 us (0.62); the launches traced: 162 us -> 101 us
  matrix products: 33 us -> 0 us
  Pallas kernels: 115 us -> 99.1 us
  other arithmetic: 6.61 us -> 0 us
  local copies, waits for them, and re-layouts: 6.23 us -> 2.36 us
    dot_general x9 -> x0, matrix products: 33 us -> none  [the longest x3 13.5 us: on_device(): jnp.dot(panel, upper_tri, precision=PRECISE, preferred_element_type=jnp.f...]
    pallas_call x4 -> x1, Pallas kernels: 115 us -> 99.1 us  [on_device(): pl.pallas_call(functools.partial(factor_kernel, prow_count, pcol_count, s...]
    gather x1 -> x0, local copies, waits for them, and re-layouts: 4.8 us -> none  [on_device(): tile = strip.at[place].get(mode='promise_in_bounds')]
    scatter x3 -> x0, other arithmetic: 3.83 us -> none  [on_device(): base = tile.at[row_start:row_start + width].set(stored)]
    unnamed x10 -> x1, local copies, waits for them, and re-layouts: 0.61 us -> 2.36 us
    reduce_sum x3 -> x0, other arithmetic: 1.71 us -> none  [before_step(): return rows + jnp.sum(moved_in + moved_out, axis=1, dtype=jnp.int32)]
where the time goes in v1:
time: 102 us; the launch traced here: 101 us
  Pallas kernels  99.1 us (97%)
  local copies, waits for them, and re-layouts  2.36 us (2%)
    pallas_call x1, Pallas kernels, on_device(): pl.pallas_call(functools.partial(factor_kernel, prow_count, pcol_count, s...  99.1 us
    unnamed x1, local copies, waits for them, and re-layouts  2.36 us

profile of v1, /device:TPU:26, one launch (start us, length us, event | category | flops | bytes accessed | tf_op | source)
XLA Modules:
  0.0 101.4 jit_solution(870322551683633410)
XLA Ops:
  0.0 99.1 %shard_map.46 = f32[768,384]{1,0:T(8,128)} custom-call(f32[768,384]{1,0:T(8,128)} %bitcast.3, s32[3,384]{1,0:T(4,128)} %pivots_ref.1, f32[3,384,384]{2,1,0:T(8,128)} %lower_ref.1, f32[3,384,384]{2,1,0:T(8,128)} %upper_ref.1), custom_call_target="tpu_custom_call" | custom-call | tf_op jit(solution)/shard_map/pallas_call | solution.py:653
  99.1 2.4 %copy.6 = f32[1,1,768,384]{3,2,1,0:T(8,128)} copy(f32[1,1,768,384]{3,2,1,0:T(8,128)} %bitcast.2) | data formatting | bytes 2359296

commit v2 on v1

--- a/solution.py
+++ b/solution.py
@@ -11,7 +11,9 @@
 CORES = 2
 F32 = jnp.float32
 BF16 = jnp.bfloat16
-HOP = 2
+HOP = 3
+EARLY = 4
+LAG = 2
 
 
 def grid_width(count):
@@ -74,49 +76,55 @@
     ]
 
 
-def tree_sends(pcol, pcol_count, source, first_axis):
-    width = grid_width(pcol_count)
-    height = pcol_count // width
-    ways = grid_ways(pcol, pcol_count)
-    pos = (pcol // width, pcol % width)
-    src = (source // width, source % width)
-    extent = (height, width)
-    a, b = first_axis, 1 - first_axis
-    away = {0: ways[0:2], 1: ways[2:4]}
-    near = src[a] + 1 if src[a] + 1 < extent[a] else src[a] - 1
-    trunk = pos[b] == src[b]
-    off_row = pos[a] != src[a]
-    sends = {}
-    if extent[a] == 1:
-        sends[a] = [pos[a] < 0, pos[a] < 0]
-        sends[b] = [pos[b] >= src[b], pos[b] <= src[b]]
-    else:
-        back_up = both(pos[a] == near, jnp.logical_not(trunk))
-        up = both(trunk, pos[a] >= src[a])
-        down = both(trunk, pos[a] <= src[a])
-        if near > src[a]:
-            down = jnp.logical_or(down, back_up)
-        else:
-            up = jnp.logical_or(up, back_up)
-        sends[a] = [up, down]
-        sends[b] = [both(off_row, pos[b] >= src[b]), both(off_row, pos[b] <= src[b])]
-    out = []
-    for axis in (0, 1):
-        for way in (0, 1):
-            out.append((both(away[axis][way][0], sends[axis][way]), away[axis][way][1]))
-    return out
-
-
-def tree_hops(pcol, pcol_count, source, first_axis):
+def tree_plan(pcol_count, source, first_axis):
     width = grid_width(pcol_count)
     extent = (pcol_count // width, width)
-    pos = (pcol // width, pcol % width)
     src = (source // width, source % width)
     a, b = first_axis, 1 - first_axis
-    straight = jnp.abs(pos[a] - src[a]) + jnp.abs(pos[b] - src[b])
-    if extent[a] == 1:
-        return straight
-    return straight + jnp.where(both(pos[a] == src[a], pos[b] != src[b]), 2, 0)
+    near = src[a] + 1 if src[a] + 1 < extent[a] else src[a] - 1
+
+    def toward(at, goal):
+        return at + (goal > at) - (goal < at)
+
+    parent = {}
+    for node in range(pcol_count):
+        pos = [node // width, node % width]
+        if node == source:
+            continue
+        if pos[b] == src[b]:
+            pos[a] = toward(pos[a], src[a])
+        elif pos[a] != src[a] or extent[a] == 1:
+            pos[b] = toward(pos[b], src[b])
+        else:
+            pos[a] = near
+        parent[node] = pos[0] * width + pos[1]
+    hops, used = {source: 0}, set()
+    for node in range(pcol_count):
+        path = [node]
+        while path[-1] != source:
+            path.append(parent[path[-1]])
+        hops[node] = len(path) - 1
+        if node > source:
+            used.update(path)
+    steps = (width, -width, 1, -1)
+    senders = [
+        [parent[c] for c in used if c != source and c - parent[c] == step]
+        if step not in steps[:way] else []
+        for way, step in enumerate(steps)
+    ]
+    return hops, used - {source}, senders
+
+
+def pick_static(index, table):
+    out = jnp.int32(0)
+    for key, value in table.items():
+        out = jnp.where(index == key, value, out)
+    return out
+
+
+def among(index, members):
+    mask = sum(1 << member for member in set(members))
+    return (lax.shift_right_logical(jnp.int32(mask), index) & 1) == 1
 
 
 class Flow:
@@ -181,8 +189,8 @@
 
 def factor_kernel(
     prow_count, pcol_count, sections, width, blocks,
-    tile_ref, pivots_ref, lower_ref, upper_ref, out_ref,
-    first, pivot, low_in, up_in, parts, top, top_parts, picked, picked_in,
+    tile_ref, pivots_ref, lower_ref, upper_ref, final_ref,
+    out_ref, first, pivot, low_in, up_in, parts, top, top_parts, picked, picked_in,
     row_panel, col_panel, row_stack, low_wide, up_stack, core_stack,
     local_sem, top_send, top_recv, pick_send, pick_recv,
     row_send, row_recv, col_send, col_recv,
@@ -289,9 +297,8 @@
         ],
         axis=1,
     )
-    for s in range(sections):
-
-        def pick(i, carry, s=s):
+    def pick_rows(s):
+        def pick(i, carry):
             start = i * step_rows
             at = pl.ds(pl.multiple_of(start, step_rows), step_rows)
             rows = jnp.sum(
@@ -307,7 +314,7 @@
         lax.fori_loop(0, tiles, pick, 0)
 
         @pl.when(core != s % CORES)
-        def _(s=s):
+        def _():
             pick_copy(s, 0, 0, partner).start()
 
     def add_in(s, slot):
@@ -344,10 +351,13 @@
                 pick_copy(s, 2, 1, {"prow": prow - CORES}).start()
 
     def urgent(s):
-        return pcol > 0 if s == 0 else pcol == 0
-
-    for s in range(sections):
-        pass_picked(s, urgent(s))
+        return pcol > 0 if s == 0 else both(pcol >= 0, s >= CORES) | (pcol == 0)
+
+    pick_rows(0)
+    for s in range(1, sections):
+        pick_rows(s)
+        pass_picked(s - 1, urgent(s - 1))
+    pass_picked(sections - 1, urgent(sections - 1))
 
     @pl.when(owns_row)
     def _():
@@ -451,23 +461,20 @@
 
         lax.fori_loop(0, tiles, place, 0)
 
-    for block in range(1, blocks):
-        settle(block)
-
-    @pl.when(jnp.logical_not(owns_row))
-    def _():
-        settle(0)
-
-    sends = [
-        [tree_sends(pcol, pcol_count, s, k) for k in range(2)] for s in range(sections)
-    ]
+    ways = grid_ways(pcol, pcol_count)
+    plans = [[tree_plan(pcol_count, s, k) for k in range(2)] for s in range(sections)]
+    sends = [[[among(pcol, who) for who in plan[2]] for plan in pair] for pair in plans]
+    gets = [[among(pcol, plan[1]) for plan in pair] for pair in plans]
+
+    def farthest(s, node):
+        return max(plan[0][node] for plan in plans[s])
 
     def live(s):
         return jnp.where(prow > s, blocks, blocks - 1)
 
     def place_of(s, i):
         turn = lax.div(i, per_block)
-        block = blocks - 1 - turn if s == 0 else blocks - live(s) + turn
+        block = blocks - live(s) + turn
         return block * width + (i - turn * per_block) * span
 
     def col_copy(s, k, i, way):
@@ -476,96 +483,121 @@
         return pltpu.make_async_remote_copy(
             src_ref=col_panel.at[s, piece],
             dst_ref=col_panel.at[s, piece],
-            send_sem=col_send.at[s, k, way, i],
+            send_sem=col_send.at[s, k, way],
             recv_sem=col_recv.at[s, k, i],
-            device_id=sends[s][k][way][1],
+            device_id=ways[way][1],
             device_id_type=MESH,
         )
 
     def col_start(s, k, i):
         for way in range(4):
 
-            @pl.when(sends[s][k][way][0])
+            @pl.when(sends[s][k][way])
             def _(way=way):
                 col_copy(s, k, i, way).start()
 
     def update(s, at):
-        return out_ref[at, :] - dot(wide(col_panel[s, at, :]), row_stack[...])
-
-    def produce(s, start, stop, updated):
+        return out_ref[at, :] - dot(wide(col_panel[s, at, :]), row_stack[s])
+
+    def rows_of(s, i):
+        return pl.ds(pl.multiple_of(place_of(s, i), span), span)
+
+    def produce(s, i, value):
+        at = rows_of(s, i)
+        value = dot(wide(value), up_stack[...])
+        col_panel[s, at, :] = value
+        out_ref[at, :] = value
+
+    def start_both(s, i):
+        for k in range(2):
+            col_start(s, k, i)
+
+    def produce_first(start, stop):
         def body(i, carry):
-            at = pl.ds(pl.multiple_of(place_of(s, i), span), span)
-            value = update(s - 1, at) if updated else out_ref[at, :]
-            value = dot(wide(value), up_stack[...])
-            col_panel[s, at, :] = value
-            out_ref[at, :] = value
+            produce(0, i, out_ref[rows_of(0, i), :])
 
             @pl.when(i > start)
             def _():
-                for k in range(2):
-                    col_start(s, k, i - 1)
+                start_both(0, i - 1)
 
             return carry
 
         lax.fori_loop(start, stop, body, 0)
-        for k in range(2):
-            col_start(s, k, stop - 1)
-
-    def relay(s, hook):
-        hops = [tree_hops(pcol, pcol_count, s, k) for k in range(2)]
-        late = [HOP * jnp.maximum(hops[k] - hops[1 - k], 0) for k in range(2)]
-        count = live(s) * per_block
-
-        def body(t, carry):
-            for k in range(2):
-                i = t - late[k]
-
-                @pl.when(both(i >= 0, i < count))
-                def _(k=k, i=i):
-                    col_copy(s, k, i, 0).wait_recv()
-                    col_start(s, k, i)
-
-            return carry
-
-        lax.fori_loop(0, per_block, body, 0)
-        hook()
-        lax.fori_loop(per_block, count + late[0] + late[1], body, 0)
-
-    def update_block(s, block):
-        def body(i, carry):
-            at = pl.ds(pl.multiple_of(block * width + i * step_rows, step_rows), step_rows)
-            out_ref[at, :] = update(s, at)
-            return carry
-
-        lax.fori_loop(0, tiles, body, 0)
+        start_both(0, stop - 1)
+
+    def forwards(s):
+        return both(core == s % CORES, prow != s)
+
+    def pass_row(s):
+        for chunk in range(tiles):
+            row_flows[s].pass_on(chunk)
+
+    def take_row(s):
+        @pl.when(jnp.logical_not(forwards(s)))
+        def _():
+            pass_row(s)
+
+        def cut(i, carry):
+            at = pl.ds(pl.multiple_of(i * step_rows, step_rows), step_rows)
+            stack(row_stack.at[s], i, row_panel[s, at, :])
+            return carry
+
+        lax.fori_loop(0, tiles, cut, 0)
 
     @pl.when(pcol == 0)
     def _():
-        produce(0, 0, (blocks - 1) * per_block, False)
-        for s in range(sections):
+        @pl.when(jnp.logical_not(owns_row))
+        def _():
+            settle(0)
+            produce_first(0, per_block)
+
+        for block in range(1, blocks):
+            settle(block)
+        for s in range(1, sections):
 
             @pl.when(prow == s)
             def _(s=s):
                 take_picked(s)
 
-        @pl.when(prow > 0)
-        def _():
-            produce(0, (blocks - 1) * per_block, blocks * per_block, False)
-
+        produce_first(jnp.where(owns_row, 0, per_block), live(0) * per_block)
+
+    @pl.when(pcol > 0)
+    def _():
+        for block in range(1, blocks):
+            settle(block)
+
+        @pl.when(jnp.logical_not(owns_row))
+        def _():
+            settle(0)
+
+    begin, begin_of, lates, computes, counts = jnp.int32(0), [], [], [], []
+    forward_at = []
     for s in range(sections):
-
-        @pl.when(pcol != s)
-        def _(s=s):
-            def hook():
-                @pl.when(pcol > s)
-                def _():
-                    for chunk in range(tiles):
-                        row_flows[s].pass_on(chunk)
-
-            relay(s, hook)
-
-        @pl.when(pcol > s)
-        def _(s=s):
+        counts.append(live(s) * per_block)
+        begin_of.append(begin)
+        lates.append(
+            [begin + pick_static(pcol, {n: HOP * h for n, h in plan[0].items()}) for plan in plans[s]]
+        )
+        lag = {n: HOP * farthest(s, n) + (LAG if n != s + 1 else 0) for n in range(pcol_count)}
+        early = {n: HOP * farthest(s, n) - EARLY for n in range(pcol_count)}
+        forward_at.append(begin + pick_static(pcol, early))
+        computes.append(begin + pick_static(pcol, lag))
+        if s + 1 < sections:
+            begin = begin + HOP * farthest(s, s + 1) + 1
+            begin = begin + jnp.where(prow == s + 1, per_block, 0)
+            for n in range(s + 2, pcol_count):
+                ahead = HOP * (farthest(s, s + 1) + farthest(s + 1, n) - farthest(s, n))
+                assert ahead + 1 >= (LAG if n == s + 2 else 0)
+
+    def inline(s):
+        return both(pcol > s, x == s // CORES) if s + 1 == sections else pcol > s
+
+    def compute(s, j):
+        last = s + 1 == sections
+        skip = 0 if last else counts[s] - counts[s + 1]
+
+        @pl.when(j == 0)
+        def _():
             if s == 0:
                 for other in range(1, sections):
 
@@ -573,41 +605,87 @@
                     def _(other=other):
                         take_picked(other)
 
-            def cut(i, carry):
-                at = pl.ds(pl.multiple_of(i * step_rows, step_rows), step_rows)
-                stack(row_stack, i, row_panel[s, at, :])
-                return carry
-
-            lax.fori_loop(0, tiles, cut, 0)
-            last = s + 1 == sections
-
-            def plain():
-                @pl.when(prow > s)
-                def _():
-                    update_block(s, 0)
-
-                if not last:
-
-                    @pl.when(prow == s + 1)
-                    def _():
-                        row_product(s + 1)
-
-                for block in range(1, blocks):
-                    update_block(s, block)
-
-            if last:
-                plain()
-            else:
-                pl.when(pcol > s + 1)(plain)
-
-                @pl.when(pcol == s + 1)
-                def _():
-                    produce(s + 1, 0, live(s + 1) * per_block, True)
-
-                    @pl.when(prow == s + 1)
-                    def _():
-                        update_block(s, 0)
-
+            take_row(s)
+
+        at = rows_of(s, j)
+        value = update(s, at)
+        if last:
+            out_ref[at, :] = value
+            return
+        makes = both(pcol == s + 1, j >= skip)
+
+        @pl.when(jnp.logical_not(makes))
+        def _():
+            out_ref[at, :] = value
+
+        @pl.when(makes)
+        def _():
+            produce(s + 1, j - skip, value)
+
+        @pl.when(both(prow == s + 1, pcol > s + 1, j == per_block - 1))
+        def _():
+            row_product(s + 1)
+
+    def turn(t, carry):
+        for s in range(sections):
+            for k in range(2):
+                i = t - lates[s][k]
+
+                @pl.when(both(gets[s][k], i >= 0, i < counts[s]))
+                def _(s=s, k=k, i=i):
+                    col_copy(s, k, i, 0).wait_recv()
+                    col_start(s, k, i)
+
+            @pl.when(both(inline(s), forwards(s), t == jnp.maximum(forward_at[s], 0)))
+            def _(s=s):
+                pass_row(s)
+
+            if s > 0:
+                i = t - begin_of[s]
+
+                @pl.when(both(pcol == s, i >= 0, i < counts[s]))
+                def _(s=s, i=i):
+                    start_both(s, i)
+
+            j = t - computes[s]
+
+            @pl.when(both(inline(s), j >= 0, j < counts[s]))
+            def _(s=s, j=j):
+                compute(s, j)
+
+        return carry
+
+    stop = jnp.int32(0)
+    for s in range(sections):
+        stop = jnp.maximum(stop, jnp.where(inline(s), computes[s] + counts[s], 0))
+        for k in range(2):
+            stop = jnp.maximum(stop, jnp.where(gets[s][k], lates[s][k] + counts[s], 0))
+        if s > 0:
+            stop = jnp.maximum(stop, jnp.where(pcol == s, begin_of[s] + counts[s], 0))
+    lax.fori_loop(0, stop, turn, 0)
+    last = sections - 1
+
+    @pl.when(both(pcol > last, jnp.logical_not(inline(last))))
+    def _():
+        @pl.when(forwards(last))
+        def _():
+            pass_row(last)
+
+        take_row(last)
+
+        def body(i, carry):
+            at = pl.ds(pl.multiple_of(i * step_rows, step_rows), step_rows)
+            out_ref[at, :] = update(last, at)
+            return carry
+
+        lax.fori_loop((blocks - live(last)) * tiles, blocks * tiles, body, 0)
+
+    @pl.when(both(prow == 0, pcol == 0))
+    def _():
+        take_picked(0)
+
+    save = pltpu.make_async_copy(out_ref, final_ref, local_sem.at[0])
+    save.start()
     for s in range(sections):
         for chunk in range(tiles):
             top_flows[s].finish(chunk)
@@ -629,14 +707,21 @@
 
         for k in range(2):
             for way in range(4):
-
-                @pl.when(sends[s][k][way][0])
-                def _(s=s, k=k, way=way):
-                    def body(i, carry):
-                        col_copy(s, k, i, way).wait_send()
-                        return carry
-
-                    lax.fori_loop(0, live(s) * per_block, body, 0)
+                for count in (blocks - 1, blocks):
+
+                    @pl.when(both(sends[s][k][way], live(s) == count))
+                    def _(s=s, k=k, way=way, count=count):
+                        piece = pl.ds(0, count * width // 2)
+                        pltpu.make_async_remote_copy(
+                            src_ref=col_panel.at[s, piece],
+                            dst_ref=col_panel.at[s, piece],
+                            send_sem=col_send.at[s, k, way],
+                            recv_sem=col_recv.at[s, k, 0],
+                            device_id=ways[way][1],
+                            device_id_type=MESH,
+                        ).wait_send()
+
+    save.wait()
 
 
 def on_device(matrix, pivots, lower_inv, upper_inv):
@@ -654,8 +739,9 @@
         functools.partial(factor_kernel, prow_count, pcol_count, sections, width, blocks),
         out_shape=jax.ShapeDtypeStruct(tile.shape, tile.dtype),
         in_specs=[pl.BlockSpec(memory_space=pl.ANY)] * 4,
-        out_specs=pl.BlockSpec(memory_space=pltpu.VMEM),
+        out_specs=pl.BlockSpec(memory_space=pl.ANY),
         scratch_shapes=[
+            pltpu.VMEM((rows, width), F32),
             pltpu.VMEM((rows, width), F32),
             pltpu.VMEM(pivots.shape, jnp.int32),
             pltpu.VMEM((width, width), F32),
@@ -667,7 +753,7 @@
             pltpu.VMEM((sections, 3, width, width), F32),
             pltpu.VMEM((sections, width, width), F32),
             pltpu.VMEM((sections, rows, width), F32),
-            pltpu.VMEM((3 * width, width), BF16),
+            pltpu.VMEM((sections, 3 * width, width), BF16),
             pltpu.VMEM((width, 3 * width), BF16),
             pltpu.VMEM((3 * width, width), BF16),
             pltpu.VMEM((3 * width, width), BF16),
@@ -678,7 +764,7 @@
             dma((sections, 3)),
             dma((sections, 3, tiles)),
             dma((sections, tiles)),
-            dma((sections, 2, 4, relays)),
+            dma((sections, 2, 4)),
             dma((sections, 2, relays)),
         ],
         compiler_params=pltpu.CompilerParams(

time: 102 us -> 84.2 us (0.83)
  Pallas kernels: 99.1 us -> 81.3 us
    pallas_call x1, Pallas kernels: 99.1 us -> 81.3 us  [on_device(): pl.pallas_call(functools.partial(factor_kernel, prow_count, pcol_count, s...]
where the time goes in v2:
time: 84.2 us; the launch traced here: 83.7 us
  Pallas kernels  81.3 us (97%)
  local copies, waits for them, and re-layouts  2.36 us (3%)
    pallas_call x1, Pallas kernels, on_device(): pl.pallas_call(functools.partial(factor_kernel, prow_count, pcol_count, s...  81.3 us
    unnamed x1, local copies, waits for them, and re-layouts  2.36 us

profile of v2, /device:TPU:26, one launch (start us, length us, event | category | flops | bytes accessed | tf_op | source)
XLA Modules:
  0.0 83.7 jit_solution(1760417103707298903)
XLA Ops:
  0.0 81.3 %shard_map.46 = f32[768,384]{1,0:T(8,128)} custom-call(f32[768,384]{1,0:T(8,128)} %bitcast.3, s32[3,384]{1,0:T(4,128)} %pivots_ref.1, f32[3,384,384]{2,1,0:T(8,128)} %lower_ref.1, f32[3,384,384]{2,1,0:T(8,128)} %upper_ref.1), custom_call_target="tpu_custom_call" | custom-call | tf_op jit(solution)/shard_map/pallas_call | solution.py:738
  81.3 2.4 %copy.6 = f32[1,1,768,384]{3,2,1,0:T(8,128)} copy(f32[1,1,768,384]{3,2,1,0:T(8,128)} %bitcast.2) | data formatting | bytes 2359296

commit v3 on v2

--- a/solution.py
+++ b/solution.py
@@ -12,7 +12,8 @@
 F32 = jnp.float32
 BF16 = jnp.bfloat16
 HOP = 3
-EARLY = 4
+EARLY = (4, 0)
+PICK = 384
 LAG = 2
 
 
@@ -250,8 +251,8 @@
     def lanes(count):
         return lax.broadcasted_iota(jnp.int32, (1, count), 1).astype(F32)
 
-    def column(start):
-        ids = lax.broadcasted_iota(jnp.int32, (step_rows, 1), 0)
+    def column(start, rows=step_rows):
+        ids = lax.broadcasted_iota(jnp.int32, (rows, 1), 0)
         return (ids + start).astype(F32)
 
     def pivot_row(s):
@@ -299,10 +300,10 @@
     )
     def pick_rows(s):
         def pick(i, carry):
-            start = i * step_rows
-            at = pl.ds(pl.multiple_of(start, step_rows), step_rows)
+            start = i * PICK
+            at = pl.ds(pl.multiple_of(start, PICK), PICK)
             rows = jnp.sum(
-                jnp.where(column(start) == lanes(width), pivot_row(s), F32(0)),
+                jnp.where(column(start, PICK) == lanes(width), pivot_row(s), F32(0)),
                 axis=1, keepdims=True,
             )
             chosen = one_hot(undo(rows, s), held_ids)
@@ -311,7 +312,7 @@
             )
             return carry
 
-        lax.fori_loop(0, tiles, pick, 0)
+        lax.fori_loop(0, width // PICK, pick, 0)
 
         @pl.when(core != s % CORES)
         def _():
@@ -353,11 +354,19 @@
     def urgent(s):
         return pcol > 0 if s == 0 else both(pcol >= 0, s >= CORES) | (pcol == 0)
 
-    pick_rows(0)
-    for s in range(1, sections):
-        pick_rows(s)
-        pass_picked(s - 1, urgent(s - 1))
-    pass_picked(sections - 1, urgent(sections - 1))
+    def pick_all(order):
+        for s in order:
+            pick_rows(s)
+            pass_picked(s, urgent(s))
+
+    @pl.when(pcol == 0)
+    def _():
+        pick_all([*range(1, sections), 0])
+
+    @pl.when(pcol > 0)
+    def _():
+        pick_all([*range(sections)])
+
 
     @pl.when(owns_row)
     def _():
@@ -393,17 +402,6 @@
             return carry
 
         lax.fori_loop(0, tiles, prepare, 0)
-
-    for chunk in range(tiles):
-        for flow in top_flows:
-            flow.pass_on(chunk)
-    for s in range(sections):
-
-        @pl.when(prow == s)
-        def _(s=s):
-            pltpu.make_async_copy(
-                tile_ref.at[pl.ds(0, width)], top.at[pl.ds(s * width, width)], local_sem.at[4]
-            ).wait()
 
     def take_picked(s):
         owner = s // CORES
@@ -413,53 +411,6 @@
         if owner < chips - 1:
             add_in(s, 2)
         out_ref[pl.ds(0, width), :] = picked[s]
-
-    def row_product(s):
-        def cut(i, carry):
-            at = pl.ds(pl.multiple_of(i * step_rows, step_rows), step_rows)
-            stack(core_stack, i, out_ref[at, :])
-            return carry
-
-        lax.fori_loop(0, tiles, cut, 0)
-        for chunk in range(tiles):
-            at = pl.ds(chunk * step_rows, step_rows)
-            value = dot(low_wide[at, :], core_stack[...])
-            row_panel[s, at, :] = value
-            out_ref[at, :] = value
-            if chunk > 0:
-                row_flows[s].send(chunk - 1, row_panel.at[s])
-        row_flows[s].send(tiles - 1, row_panel.at[s])
-
-    @pl.when(both(prow == 0, pcol > 0))
-    def _():
-        take_picked(0)
-        row_product(0)
-
-    for s in range(sections):
-        pass_picked(s, jnp.logical_not(urgent(s)))
-
-    def cut_top(i, carry):
-        at = pl.ds(pl.multiple_of(i * step_rows, step_rows), step_rows)
-        for k, part in enumerate(split3(top[at, :])):
-            top_parts[k, at, :] = part
-        return carry
-
-    lax.fori_loop(0, tiles * sections, cut_top, 0)
-
-    def settle(block):
-        def place(i, carry):
-            start = i * step_rows
-            at = pl.ds(pl.multiple_of(block * width + start, step_rows), step_rows)
-            rows = column(start + (block * prow_count + prow) * width)
-            rows = undo(rows, sections)
-            chosen = one_hot(rows, lanes(sections * width))
-            value = (
-                dot(chosen, top_parts[2]) + dot(chosen, top_parts[1]) + dot(chosen, top_parts[0])
-            )
-            out_ref[at, :] = jnp.where(rows < F32(sections * width), value, first[at, :])
-            return carry
-
-        lax.fori_loop(0, tiles, place, 0)
 
     ways = grid_ways(pcol, pcol_count)
     plans = [[tree_plan(pcol_count, s, k) for k in range(2)] for s in range(sections)]
@@ -525,6 +476,71 @@
         lax.fori_loop(start, stop, body, 0)
         start_both(0, stop - 1)
 
+    for s in range(1, min(CORES, sections)):
+
+        @pl.when(both(pcol == 0, prow == s))
+        def _(s=s):
+            take_picked(s)
+            produce_first(0, per_block)
+
+    for chunk in range(tiles):
+        for flow in top_flows:
+            flow.pass_on(chunk)
+    for s in range(sections):
+
+        @pl.when(prow == s)
+        def _(s=s):
+            pltpu.make_async_copy(
+                tile_ref.at[pl.ds(0, width)], top.at[pl.ds(s * width, width)], local_sem.at[4]
+            ).wait()
+
+    def row_product(s):
+        def cut(i, carry):
+            at = pl.ds(pl.multiple_of(i * step_rows, step_rows), step_rows)
+            stack(core_stack, i, out_ref[at, :])
+            return carry
+
+        lax.fori_loop(0, tiles, cut, 0)
+        for chunk in range(tiles):
+            at = pl.ds(chunk * step_rows, step_rows)
+            value = dot(low_wide[at, :], core_stack[...])
+            row_panel[s, at, :] = value
+            out_ref[at, :] = value
+            if chunk > 0:
+                row_flows[s].send(chunk - 1, row_panel.at[s])
+        row_flows[s].send(tiles - 1, row_panel.at[s])
+
+    @pl.when(both(prow == 0, pcol > 0))
+    def _():
+        take_picked(0)
+        row_product(0)
+
+    for s in range(sections):
+        pass_picked(s, jnp.logical_not(urgent(s)))
+
+    def cut_top(i, carry):
+        at = pl.ds(pl.multiple_of(i * step_rows, step_rows), step_rows)
+        for k, part in enumerate(split3(top[at, :])):
+            top_parts[k, at, :] = part
+        return carry
+
+    lax.fori_loop(0, tiles * sections, cut_top, 0)
+
+    def settle(block):
+        def place(i, carry):
+            start = i * PICK
+            at = pl.ds(pl.multiple_of(block * width + start, PICK), PICK)
+            rows = column(start + (block * prow_count + prow) * width, PICK)
+            rows = undo(rows, sections)
+            chosen = one_hot(rows, lanes(sections * width))
+            value = (
+                dot(chosen, top_parts[2]) + dot(chosen, top_parts[1]) + dot(chosen, top_parts[0])
+            )
+            out_ref[at, :] = jnp.where(rows < F32(sections * width), value, first[at, :])
+            return carry
+
+        lax.fori_loop(0, width // PICK, place, 0)
+
     def forwards(s):
         return both(core == s % CORES, prow != s)
 
@@ -553,13 +569,15 @@
 
         for block in range(1, blocks):
             settle(block)
-        for s in range(1, sections):
-
-            @pl.when(prow == s)
-            def _(s=s):
-                take_picked(s)
-
-        produce_first(jnp.where(owns_row, 0, per_block), live(0) * per_block)
+        for s in range(sections):
+            if s == 0 or s >= CORES:
+
+                @pl.when(prow == s)
+                def _(s=s):
+                    take_picked(s)
+
+        done = jnp.logical_or(both(prow > 0, prow < CORES), jnp.logical_not(owns_row))
+        produce_first(jnp.where(done, per_block, 0), live(0) * per_block)
 
     @pl.when(pcol > 0)
     def _():
@@ -579,7 +597,7 @@
             [begin + pick_static(pcol, {n: HOP * h for n, h in plan[0].items()}) for plan in plans[s]]
         )
         lag = {n: HOP * farthest(s, n) + (LAG if n != s + 1 else 0) for n in range(pcol_count)}
-        early = {n: HOP * farthest(s, n) - EARLY for n in range(pcol_count)}
+        early = {n: HOP * farthest(s, n) - EARLY[min(s, 1)] for n in range(pcol_count)}
         forward_at.append(begin + pick_static(pcol, early))
         computes.append(begin + pick_static(pcol, lag))
         if s + 1 < sections:
@@ -590,7 +608,7 @@
                 assert ahead + 1 >= (LAG if n == s + 2 else 0)
 
     def inline(s):
-        return both(pcol > s, x == s // CORES) if s + 1 == sections else pcol > s
+        return pcol < 0 if s + 1 == sections else pcol > s
 
     def compute(s, j):
         last = s + 1 == sections
@@ -674,15 +692,11 @@
         take_row(last)
 
         def body(i, carry):
-            at = pl.ds(pl.multiple_of(i * step_rows, step_rows), step_rows)
+            at = pl.ds(pl.multiple_of(i * width, width), width)
             out_ref[at, :] = update(last, at)
             return carry
 
-        lax.fori_loop((blocks - live(last)) * tiles, blocks * tiles, body, 0)
-
-    @pl.when(both(prow == 0, pcol == 0))
-    def _():
-        take_picked(0)
+        lax.fori_loop(blocks - live(last), blocks, body, 0)
 
     save = pltpu.make_async_copy(out_ref, final_ref, local_sem.at[0])
     save.start()
@@ -735,6 +749,7 @@
     tiles = 3
     relays = blocks * 6
     dma = pltpu.SemaphoreType.DMA
+    args = (tile, pivots, lower_inv, upper_inv)
     out = pl.pallas_call(
         functools.partial(factor_kernel, prow_count, pcol_count, sections, width, blocks),
         out_shape=jax.ShapeDtypeStruct(tile.shape, tile.dtype),
@@ -768,9 +783,9 @@
             dma((sections, 2, relays)),
         ],
         compiler_params=pltpu.CompilerParams(
-            collective_id=0, has_side_effects=True, vmem_limit_bytes=60 * 1024 * 1024
+            collective_id=0, has_side_effects=True, vmem_limit_bytes=40 * 1024 * 1024
         ),
-    )(tile, pivots, lower_inv, upper_inv)
+    )(*[pltpu.with_memory_space_constraint(v, pltpu.HBM) for v in args])
     return out[None, None]
 
 

time: 84.2 us -> 77.7 us (0.923)
  Pallas kernels: 81.3 us -> 76.6 us
  local copies, waits for them, and re-layouts: 2.36 us -> 1.02 us
    pallas_call x1, Pallas kernels: 81.3 us -> 76.6 us  [on_device(): pl.pallas_call(functools.partial(factor_kernel, prow_count, pcol_count, s...]
    unnamed x1, local copies, waits for them, and re-layouts: 2.36 us -> 1.02 us
where the time goes in v3:
time: 77.7 us; the launch traced here: 77.6 us
  Pallas kernels  76.6 us (99%)
  local copies, waits for them, and re-layouts  1.02 us (1%)
    pallas_call x1, Pallas kernels, on_device(): pl.pallas_call(functools.partial(factor_kernel, prow_count, pcol_count, s...  76.6 us

profile of v3, /device:TPU:26, one launch (start us, length us, event | category | flops | bytes accessed | tf_op | source)
XLA Modules:
  0.0 77.6 jit_solution(244259532340954673)
XLA Ops:
  0.0 76.6 %shard_map.46 = f32[768,384]{1,0:T(8,128)S(1)} custom-call(f32[768,384]{1,0:T(8,128)} %bitcast.3, s32[3,384]{1,0:T(4,128)} %pivots_ref.1, f32[3,384,384]{2,1,0:T(8,128)} %lower_ref.1, f32[3,384,384]{2,1,0:T(8,128)} %upper_ref.1), custom_call_target="tpu_custom_call" | custom-call | tf_op jit(solution)/shard_map/pallas_call | solution.py:753
  76.6 1.0 %copy.6 = f32[1,1,768,384]{3,2,1,0:T(8,128)} copy(f32[1,1,768,384]{3,2,1,0:T(8,128)S(1)} %bitcast.2) | data formatting | bytes 2359296

commit v4 on v3

--- a/solution.py
+++ b/solution.py
@@ -13,7 +13,9 @@
 BF16 = jnp.bfloat16
 HOP = 3
 EARLY = (4, 0)
+PARTS = 1
 PICK = 384
+PATIENCE = 4
 LAG = 2
 
 
@@ -194,7 +196,7 @@
     out_ref, first, pivot, low_in, up_in, parts, top, top_parts, picked, picked_in,
     row_panel, col_panel, row_stack, low_wide, up_stack, core_stack,
     local_sem, top_send, top_recv, pick_send, pick_recv,
-    row_send, row_recv, col_send, col_recv,
+    row_send, row_recv, col_send, col_recv, gate,
 ):
     prow = lax.axis_index("prow")
     pcol = lax.axis_index("pcol")
@@ -202,7 +204,7 @@
     chips = prow_count // CORES
     step_rows = width // 3
     tiles = width // step_rows
-    relay_rows = col_panel.shape[1] // (2 * col_recv.shape[2])
+    relay_rows = PARTS * col_panel.shape[1] // (2 * col_recv.shape[2])
     span = 2 * relay_rows
     per_block = width // span
 
@@ -238,12 +240,20 @@
 
     entry_barrier(line_ways(prow, prow_count) + grid_ways(pcol, pcol_count))
 
+    def waits_for_picks(s):
+        return prow >= 0 if s >= CORES else prow < 0
+
     for s in range(sections):
 
         @pl.when(prow == s)
         def _(s=s):
-            for chunk in range(tiles):
+            for chunk in range(tiles - 1):
                 top_flows[s].send(chunk, tile_ref)
+
+            @pl.when(jnp.logical_not(waits_for_picks(s)))
+            def _():
+                top_flows[s].send(tiles - 1, tile_ref)
+
             pltpu.make_async_copy(
                 tile_ref.at[pl.ds(0, width)], top.at[pl.ds(s * width, width)], local_sem.at[4]
             ).start()
@@ -352,7 +362,7 @@
                 pick_copy(s, 2, 1, {"prow": prow - CORES}).start()
 
     def urgent(s):
-        return pcol > 0 if s == 0 else both(pcol >= 0, s >= CORES) | (pcol == 0)
+        return pcol > 0 if s == 0 else pcol == 0
 
     def pick_all(order):
         for s in order:
@@ -366,6 +376,12 @@
     @pl.when(pcol > 0)
     def _():
         pick_all([*range(sections)])
+
+    for s in range(sections):
+
+        @pl.when(both(prow == s, waits_for_picks(s)))
+        def _(s=s):
+            top_flows[s].send(tiles - 1, tile_ref)
 
 
     @pl.when(owns_row)
@@ -428,24 +444,26 @@
         block = blocks - live(s) + turn
         return block * width + (i - turn * per_block) * span
 
-    def col_copy(s, k, i, way):
-        start = pl.multiple_of(place_of(s, i) + k * relay_rows, relay_rows)
-        piece = pl.ds(start, relay_rows)
+    part_rows = relay_rows // PARTS
+
+    def col_copy(s, k, i, h, way):
+        start = place_of(s, i) + k * relay_rows + h * part_rows
+        piece = pl.ds(pl.multiple_of(start, part_rows), part_rows)
         return pltpu.make_async_remote_copy(
             src_ref=col_panel.at[s, piece],
             dst_ref=col_panel.at[s, piece],
             send_sem=col_send.at[s, k, way],
-            recv_sem=col_recv.at[s, k, i],
+            recv_sem=col_recv.at[s, k, i * PARTS + h],
             device_id=ways[way][1],
             device_id_type=MESH,
         )
 
-    def col_start(s, k, i):
+    def col_start(s, k, i, h):
         for way in range(4):
 
             @pl.when(sends[s][k][way])
             def _(way=way):
-                col_copy(s, k, i, way).start()
+                col_copy(s, k, i, h, way).start()
 
     def update(s, at):
         return out_ref[at, :] - dot(wide(col_panel[s, at, :]), row_stack[s])
@@ -460,8 +478,9 @@
         out_ref[at, :] = value
 
     def start_both(s, i):
-        for k in range(2):
-            col_start(s, k, i)
+        for h in range(PARTS):
+            for k in range(2):
+                col_start(s, k, i, h)
 
     def produce_first(start, stop):
         def body(i, carry):
@@ -482,49 +501,54 @@
         def _(s=s):
             take_picked(s)
             produce_first(0, per_block)
-
-    for chunk in range(tiles):
-        for flow in top_flows:
-            flow.pass_on(chunk)
-    for s in range(sections):
-
-        @pl.when(prow == s)
-        def _(s=s):
-            pltpu.make_async_copy(
-                tile_ref.at[pl.ds(0, width)], top.at[pl.ds(s * width, width)], local_sem.at[4]
-            ).wait()
-
-    def row_product(s):
-        def cut(i, carry):
+            pl.semaphore_signal(gate, inc=1, device_id=partner, device_id_type=MESH)
+
+    def row_product(s, chunk):
+        at = pl.ds(chunk * step_rows, step_rows)
+        stack(core_stack, chunk, out_ref[at, :])
+        upto = (chunk + 1) * step_rows
+        value = F32(0)
+        for k in range(3):
+            upper = pl.ds(k * width, upto)
+            value = value + dot(low_wide[at, k * width : k * width + upto], core_stack[upper, :])
+        row_panel[s, at, :] = value
+        out_ref[at, :] = value
+
+    @pl.when(both(prow == 0, pcol > 0))
+    def _():
+        take_picked(0)
+        for chunk in range(tiles):
+            row_product(0, chunk)
+            if chunk > 0:
+                row_flows[0].send(chunk - 1, row_panel.at[0])
+        row_flows[0].send(tiles - 1, row_panel.at[0])
+
+    later = both(prow > 0, prow < min(CORES, sections), pcol > 0)
+
+    def land_tops():
+        for chunk in range(tiles):
+            for flow in top_flows:
+                flow.pass_on(chunk)
+            if chunk == tiles - 2:
+                for s in range(sections):
+                    pass_picked(s, jnp.logical_not(urgent(s)))
+        for s in range(sections):
+
+            @pl.when(prow == s)
+            def _(s=s):
+                pltpu.make_async_copy(
+                    tile_ref.at[pl.ds(0, width)], top.at[pl.ds(s * width, width)], local_sem.at[4]
+                ).wait()
+
+        def cut_top(i, carry):
             at = pl.ds(pl.multiple_of(i * step_rows, step_rows), step_rows)
-            stack(core_stack, i, out_ref[at, :])
+            for k, part in enumerate(split3(top[at, :])):
+                top_parts[k, at, :] = part
             return carry
 
-        lax.fori_loop(0, tiles, cut, 0)
-        for chunk in range(tiles):
-            at = pl.ds(chunk * step_rows, step_rows)
-            value = dot(low_wide[at, :], core_stack[...])
-            row_panel[s, at, :] = value
-            out_ref[at, :] = value
-            if chunk > 0:
-                row_flows[s].send(chunk - 1, row_panel.at[s])
-        row_flows[s].send(tiles - 1, row_panel.at[s])
-
-    @pl.when(both(prow == 0, pcol > 0))
-    def _():
-        take_picked(0)
-        row_product(0)
-
-    for s in range(sections):
-        pass_picked(s, jnp.logical_not(urgent(s)))
-
-    def cut_top(i, carry):
-        at = pl.ds(pl.multiple_of(i * step_rows, step_rows), step_rows)
-        for k, part in enumerate(split3(top[at, :])):
-            top_parts[k, at, :] = part
-        return carry
-
-    lax.fori_loop(0, tiles * sections, cut_top, 0)
+        lax.fori_loop(0, tiles * sections, cut_top, 0)
+
+    pl.when(jnp.logical_not(later))(land_tops)
 
     def settle(block):
         def place(i, carry):
@@ -569,17 +593,34 @@
 
         for block in range(1, blocks):
             settle(block)
-        for s in range(sections):
-            if s == 0 or s >= CORES:
-
-                @pl.when(prow == s)
-                def _(s=s):
-                    take_picked(s)
+        for s in range(CORES, sections):
+
+            @pl.when(prow == s)
+            def _(s=s):
+                take_picked(s)
+
+        if sections > 1:
+
+            @pl.when(prow == 0)
+            def _():
+                pl.semaphore_wait(gate, 1)
+
+        paired = [s for s in range(CORES, sections) if s ^ 1 >= sections]
+        for s in paired:
+
+            @pl.when(prow == s ^ 1)
+            def _():
+                pl.semaphore_wait(gate, 1)
 
         done = jnp.logical_or(both(prow > 0, prow < CORES), jnp.logical_not(owns_row))
         produce_first(jnp.where(done, per_block, 0), live(0) * per_block)
-
-    @pl.when(pcol > 0)
+        for s in paired:
+
+            @pl.when(prow == s)
+            def _():
+                pl.semaphore_signal(gate, inc=1, device_id=partner, device_id_type=MESH)
+
+    @pl.when(both(pcol > 0, jnp.logical_not(later)))
     def _():
         for block in range(1, blocks):
             settle(block)
@@ -597,15 +638,18 @@
             [begin + pick_static(pcol, {n: HOP * h for n, h in plan[0].items()}) for plan in plans[s]]
         )
         lag = {n: HOP * farthest(s, n) + (LAG if n != s + 1 else 0) for n in range(pcol_count)}
+        slack = jnp.where(x == 0, per_block, 0) if s == 0 else 0
+        rest = PATIENCE if s == 0 else 0
+        wait = jnp.where(both(prow >= CORES, prow < sections, pcol != 1), rest, 0)
         early = {n: HOP * farthest(s, n) - EARLY[min(s, 1)] for n in range(pcol_count)}
         forward_at.append(begin + pick_static(pcol, early))
-        computes.append(begin + pick_static(pcol, lag))
+        computes.append(begin + pick_static(pcol, lag) + jnp.where(pcol == s + 1, slack, wait))
         if s + 1 < sections:
-            begin = begin + HOP * farthest(s, s + 1) + 1
+            begin = begin + HOP * farthest(s, s + 1) + 1 + slack
             begin = begin + jnp.where(prow == s + 1, per_block, 0)
             for n in range(s + 2, pcol_count):
                 ahead = HOP * (farthest(s, s + 1) + farthest(s + 1, n) - farthest(s, n))
-                assert ahead + 1 >= (LAG if n == s + 2 else 0)
+                assert ahead + 1 >= (LAG if n == s + 2 else 0) + rest
 
     def inline(s):
         return pcol < 0 if s + 1 == sections else pcol > s
@@ -624,6 +668,14 @@
                         take_picked(other)
 
             take_row(s)
+
+        if s == 0:
+
+            @pl.when(both(later, j == per_block))
+            def _():
+                land_tops()
+                for block in range(1, blocks):
+                    settle(block)
 
         at = rows_of(s, j)
         value = update(s, at)
@@ -640,9 +692,21 @@
         def _():
             produce(s + 1, j - skip, value)
 
-        @pl.when(both(prow == s + 1, pcol > s + 1, j == per_block - 1))
-        def _():
-            row_product(s + 1)
+        per_tile = per_block // tiles
+        for chunk in range(tiles):
+            ready = (chunk + 1) * per_tile - 1
+
+            @pl.when(both(prow == s + 1, pcol > s + 1, j == ready))
+            def _(chunk=chunk):
+                row_product(s + 1, chunk)
+                if chunk == tiles - 1:
+                    row_flows[s + 1].send(chunk, row_panel.at[s + 1])
+
+            if chunk < tiles - 1:
+
+                @pl.when(both(prow == s + 1, pcol > s + 1, j == ready + 1))
+                def _(chunk=chunk):
+                    row_flows[s + 1].send(chunk, row_panel.at[s + 1])
 
     def turn(t, carry):
         for s in range(sections):
@@ -651,8 +715,9 @@
 
                 @pl.when(both(gets[s][k], i >= 0, i < counts[s]))
                 def _(s=s, k=k, i=i):
-                    col_copy(s, k, i, 0).wait_recv()
-                    col_start(s, k, i)
+                    for h in range(PARTS):
+                        col_copy(s, k, i, h, 0).wait_recv()
+                        col_start(s, k, i, h)
 
             @pl.when(both(inline(s), forwards(s), t == jnp.maximum(forward_at[s], 0)))
             def _(s=s):
@@ -682,6 +747,10 @@
             stop = jnp.maximum(stop, jnp.where(pcol == s, begin_of[s] + counts[s], 0))
     lax.fori_loop(0, stop, turn, 0)
     last = sections - 1
+
+    @pl.when(both(prow == 0, pcol == 0))
+    def _():
+        take_picked(0)
 
     @pl.when(both(pcol > last, jnp.logical_not(inline(last))))
     def _():
@@ -780,7 +849,8 @@
             dma((sections, 3, tiles)),
             dma((sections, tiles)),
             dma((sections, 2, 4)),
-            dma((sections, 2, relays)),
+            dma((sections, 2, relays * PARTS)),
+            pltpu.SemaphoreType.REGULAR,
         ],
         compiler_params=pltpu.CompilerParams(
             collective_id=0, has_side_effects=True, vmem_limit_bytes=40 * 1024 * 1024

time: 77.7 us -> 75.8 us (0.976)
  Pallas kernels: 76.6 us -> 74.6 us
    pallas_call x1, Pallas kernels: 76.6 us -> 74.6 us  [on_device(): pl.pallas_call(functools.partial(factor_kernel, prow_count, pcol_count, s...]
where the time goes in v4:
time: 75.8 us; the launch traced here: 75.6 us
  Pallas kernels  74.6 us (98%)
  local copies, waits for them, and re-layouts  1.02 us (1%)
    pallas_call x1, Pallas kernels, on_device(): pl.pallas_call(functools.partial(factor_kernel, prow_count, pcol_count, s...  74.6 us

profile of v4, /device:TPU:26, one launch (start us, length us, event | category | flops | bytes accessed | tf_op | source)
XLA Modules:
  0.0 75.6 jit_solution(86553935843902175)
XLA Ops:
  0.0 74.6 %shard_map.46 = f32[768,384]{1,0:T(8,128)S(1)} custom-call(f32[768,384]{1,0:T(8,128)} %bitcast.3, s32[3,384]{1,0:T(4,128)} %pivots_ref.1, f32[3,384,384]{2,1,0:T(8,128)} %lower_ref.1, f32[3,384,384]{2,1,0:T(8,128)} %upper_ref.1), custom_call_target="tpu_custom_call" | custom-call | tf_op jit(solution)/shard_map/pallas_call | solution.py:822
  74.6 1.0 %copy.6 = f32[1,1,768,384]{3,2,1,0:T(8,128)} copy(f32[1,1,768,384]{3,2,1,0:T(8,128)S(1)} %bitcast.2) | data formatting | bytes 2359296

commit v5 on v4

--- a/solution.py
+++ b/solution.py
@@ -14,7 +14,6 @@
 HOP = 3
 EARLY = (4, 0)
 PARTS = 1
-PICK = 384
 PATIENCE = 4
 LAG = 2
 
@@ -140,7 +139,7 @@
         return pltpu.make_async_remote_copy(
             src_ref=ref.at[piece],
             dst_ref=self.land_ref.at[piece],
-            send_sem=self.send_sem.at[way, chunk],
+            send_sem=self.send_sem.at[way],
             recv_sem=self.recv_sem.at[chunk],
             device_id=self.sends[way][1],
             device_id_type=MESH,
@@ -159,12 +158,20 @@
             self.copy(chunk, 0, self.land_ref).wait_recv()
             self.send(chunk, self.land_ref)
 
-    def finish(self, chunk):
-        for way, (cond, _device) in enumerate(self.sends):
+    def finish(self, count):
+        piece = pl.ds(0, count * self.rows)
+        for way, (cond, device) in enumerate(self.sends):
 
             @pl.when(cond)
-            def _(way=way):
-                self.copy(chunk, way, self.land_ref).wait_send()
+            def _(way=way, device=device):
+                pltpu.make_async_remote_copy(
+                    src_ref=self.land_ref.at[piece],
+                    dst_ref=self.land_ref.at[piece],
+                    send_sem=self.send_sem.at[way],
+                    recv_sem=self.recv_sem.at[0],
+                    device_id=device,
+                    device_id_type=MESH,
+                ).wait_send()
 
 
 def split2(value):
@@ -310,10 +317,10 @@
     )
     def pick_rows(s):
         def pick(i, carry):
-            start = i * PICK
-            at = pl.ds(pl.multiple_of(start, PICK), PICK)
+            start = i * width
+            at = pl.ds(pl.multiple_of(start, width), width)
             rows = jnp.sum(
-                jnp.where(column(start, PICK) == lanes(width), pivot_row(s), F32(0)),
+                jnp.where(column(start, width) == lanes(width), pivot_row(s), F32(0)),
                 axis=1, keepdims=True,
             )
             chosen = one_hot(undo(rows, s), held_ids)
@@ -322,7 +329,7 @@
             )
             return carry
 
-        lax.fori_loop(0, width // PICK, pick, 0)
+        lax.fori_loop(0, width // width, pick, 0)
 
         @pl.when(core != s % CORES)
         def _():
@@ -422,11 +429,21 @@
     def take_picked(s):
         owner = s // CORES
         add_in(s, 0)
-        if owner > 0:
-            add_in(s, 1)
-        if owner < chips - 1:
-            add_in(s, 2)
-        out_ref[pl.ds(0, width), :] = picked[s]
+        slots = [1] * (owner > 0) + [2] * (owner < chips - 1)
+        for slot in slots[:-1]:
+            add_in(s, slot)
+        for slot in slots[-1:]:
+            pick_copy(s, slot, 1, partner).wait_recv()
+
+        def put(i, carry):
+            at = pl.ds(pl.multiple_of(i * step_rows, step_rows), step_rows)
+            value = picked[s, at, :]
+            for slot in slots[-1:]:
+                value = value + picked_in[s, slot, at, :]
+            out_ref[at, :] = value
+            return carry
+
+        lax.fori_loop(0, tiles, put, 0)
 
     ways = grid_ways(pcol, pcol_count)
     plans = [[tree_plan(pcol_count, s, k) for k in range(2)] for s in range(sections)]
@@ -526,35 +543,37 @@
     later = both(prow > 0, prow < min(CORES, sections), pcol > 0)
 
     def land_tops():
+        for s in range(sections):
+
+            @pl.when(prow == s)
+            def _(s=s):
+                pltpu.make_async_copy(
+                    tile_ref.at[pl.ds(0, width)], top.at[pl.ds(s * width, width)], local_sem.at[4]
+                ).wait()
+
         for chunk in range(tiles):
             for flow in top_flows:
                 flow.pass_on(chunk)
             if chunk == tiles - 2:
                 for s in range(sections):
                     pass_picked(s, jnp.logical_not(urgent(s)))
-        for s in range(sections):
-
-            @pl.when(prow == s)
-            def _(s=s):
-                pltpu.make_async_copy(
-                    tile_ref.at[pl.ds(0, width)], top.at[pl.ds(s * width, width)], local_sem.at[4]
-                ).wait()
-
-        def cut_top(i, carry):
-            at = pl.ds(pl.multiple_of(i * step_rows, step_rows), step_rows)
-            for k, part in enumerate(split3(top[at, :])):
-                top_parts[k, at, :] = part
-            return carry
-
-        lax.fori_loop(0, tiles * sections, cut_top, 0)
+
+            def cut_top(s, carry, chunk=chunk):
+                start = s * width + chunk * step_rows
+                at = pl.ds(pl.multiple_of(start, step_rows), step_rows)
+                for k, part in enumerate(split3(top[at, :])):
+                    top_parts[k, at, :] = part
+                return carry
+
+            lax.fori_loop(0, sections, cut_top, 0)
 
     pl.when(jnp.logical_not(later))(land_tops)
 
-    def settle(block):
+    def settle(block, first_part=0, parts_count=1, size=width):
         def place(i, carry):
-            start = i * PICK
-            at = pl.ds(pl.multiple_of(block * width + start, PICK), PICK)
-            rows = column(start + (block * prow_count + prow) * width, PICK)
+            start = i * size
+            at = pl.ds(pl.multiple_of(block * width + start, size), size)
+            rows = column(start + (block * prow_count + prow) * width, size)
             rows = undo(rows, sections)
             chosen = one_hot(rows, lanes(sections * width))
             value = (
@@ -563,7 +582,7 @@
             out_ref[at, :] = jnp.where(rows < F32(sections * width), value, first[at, :])
             return carry
 
-        lax.fori_loop(0, width // PICK, place, 0)
+        lax.fori_loop(first_part, first_part + parts_count, place, 0)
 
     def forwards(s):
         return both(core == s % CORES, prow != s)
@@ -588,8 +607,9 @@
     def _():
         @pl.when(jnp.logical_not(owns_row))
         def _():
-            settle(0)
-            produce_first(0, per_block)
+            for half in range(2):
+                settle(0, half, 1, width // 2)
+                produce_first(half * per_block // 2, (half + 1) * per_block // 2)
 
         for block in range(1, blocks):
             settle(block)
@@ -760,23 +780,25 @@
 
         take_row(last)
 
-        def body(i, carry):
-            at = pl.ds(pl.multiple_of(i * width, width), width)
+    def save(block):
+        at = pl.ds(block * width, width)
+        return pltpu.make_async_copy(out_ref.at[at], final_ref.at[at], local_sem.at[block])
+
+    for block in range(blocks):
+
+        @pl.when(both(pcol > last, block >= blocks - live(last)))
+        def _(block=block):
+            at = pl.ds(block * width, width)
             out_ref[at, :] = update(last, at)
-            return carry
-
-        lax.fori_loop(blocks - live(last), blocks, body, 0)
-
-    save = pltpu.make_async_copy(out_ref, final_ref, local_sem.at[0])
-    save.start()
+
+        save(block).start()
+
     for s in range(sections):
-        for chunk in range(tiles):
-            top_flows[s].finish(chunk)
+        top_flows[s].finish(tiles)
 
         @pl.when(pcol > s)
         def _(s=s):
-            for chunk in range(tiles):
-                row_flows[s].finish(chunk)
+            row_flows[s].finish(tiles)
 
         owner = s // CORES
 
@@ -804,7 +826,8 @@
                             device_id_type=MESH,
                         ).wait_send()
 
-    save.wait()
+    for block in range(blocks):
+        save(block).wait()
 
 
 def on_device(matrix, pivots, lower_inv, upper_inv):
@@ -841,12 +864,12 @@
             pltpu.VMEM((width, 3 * width), BF16),
             pltpu.VMEM((3 * width, width), BF16),
             pltpu.VMEM((3 * width, width), BF16),
-            dma((5,)),
-            dma((sections, 3, tiles)),
+            dma((4 + blocks,)),
+            dma((sections, 3)),
             dma((sections, tiles)),
             dma((sections, 2)),
             dma((sections, 3)),
-            dma((sections, 3, tiles)),
+            dma((sections, 3)),
             dma((sections, tiles)),
             dma((sections, 2, 4)),
             dma((sections, 2, relays * PARTS)),

time: 75.8 us -> 75.2 us (level)
  no operation moved by 1% of the time
where the time goes in v5:
time: 75.2 us; the launch traced here: 75.1 us
  Pallas kernels  74 us (98%)
  local copies, waits for them, and re-layouts  1.02 us (1%)
    pallas_call x1, Pallas kernels, on_device(): pl.pallas_call(functools.partial(factor_kernel, prow_count, pcol_count, s...  74 us

profile of v5, /device:TPU:26, one launch (start us, length us, event | category | flops | bytes accessed | tf_op | source)
XLA Modules:
  0.0 75.1 jit_solution(6971342589553579286)
XLA Ops:
  0.0 74.0 %shard_map.46 = f32[768,384]{1,0:T(8,128)S(1)} custom-call(f32[768,384]{1,0:T(8,128)} %bitcast.3, s32[3,384]{1,0:T(4,128)} %pivots_ref.1, f32[3,384,384]{2,1,0:T(8,128)} %lower_ref.1, f32[3,384,384]{2,1,0:T(8,128)} %upper_ref.1), custom_call_target="tpu_custom_call" | custom-call | tf_op jit(solution)/shard_map/pallas_call | solution.py:845
  74.0 1.0 %copy.6 = f32[1,1,768,384]{3,2,1,0:T(8,128)} copy(f32[1,1,768,384]{3,2,1,0:T(8,128)S(1)} %bitcast.2) | data formatting | bytes 2359296

commit v6 on v5

--- a/solution.py
+++ b/solution.py
@@ -632,13 +632,17 @@
             def _():
                 pl.semaphore_wait(gate, 1)
 
-        done = jnp.logical_or(both(prow > 0, prow < CORES), jnp.logical_not(owns_row))
-        produce_first(jnp.where(done, per_block, 0), live(0) * per_block)
         for s in paired:
 
             @pl.when(prow == s)
             def _():
+                produce_first(0, per_block + per_block // 2)
                 pl.semaphore_signal(gate, inc=1, device_id=partner, device_id_type=MESH)
+
+        done = jnp.where(both(prow > 0, prow < CORES) | jnp.logical_not(owns_row), per_block, 0)
+        for s in paired:
+            done = jnp.where(prow == s, per_block + per_block // 2, done)
+        produce_first(done, live(0) * per_block)
 
     @pl.when(both(pcol > 0, jnp.logical_not(later)))
     def _():

time: 75.2 us -> 74.4 us (0.989)
  Pallas kernels: 74 us -> 73.2 us
    pallas_call x1, Pallas kernels: 74 us -> 73.2 us  [on_device(): pl.pallas_call(functools.partial(factor_kernel, prow_count, pcol_count, s...]
where the time goes in v6:
time: 74.4 us; the launch traced here: 74.2 us
  Pallas kernels  73.2 us (98%)
  local copies, waits for them, and re-layouts  1.02 us (1%)
    pallas_call x1, Pallas kernels, on_device(): pl.pallas_call(functools.partial(factor_kernel, prow_count, pcol_count, s...  73.2 us

profile of v6, /device:TPU:26, one launch (start us, length us, event | category | flops | bytes accessed | tf_op | source)
XLA Modules:
  0.0 74.2 jit_solution(6433999850196158427)
XLA Ops:
  0.0 73.2 %shard_map.46 = f32[768,384]{1,0:T(8,128)S(1)} custom-call(f32[768,384]{1,0:T(8,128)} %bitcast.3, s32[3,384]{1,0:T(4,128)} %pivots_ref.1, f32[3,384,384]{2,1,0:T(8,128)} %lower_ref.1, f32[3,384,384]{2,1,0:T(8,128)} %upper_ref.1), custom_call_target="tpu_custom_call" | custom-call | tf_op jit(solution)/shard_map/pallas_call | solution.py:849
  73.2 1.0 %copy.6 = f32[1,1,768,384]{3,2,1,0:T(8,128)} copy(f32[1,1,768,384]{3,2,1,0:T(8,128)S(1)} %bitcast.2) | data formatting | bytes 2359296

commit v7 on v6

--- a/solution.py
+++ b/solution.py
@@ -636,12 +636,12 @@
 
             @pl.when(prow == s)
             def _():
-                produce_first(0, per_block + per_block // 2)
+                produce_first(0, per_block + per_block // 3)
                 pl.semaphore_signal(gate, inc=1, device_id=partner, device_id_type=MESH)
 
         done = jnp.where(both(prow > 0, prow < CORES) | jnp.logical_not(owns_row), per_block, 0)
         for s in paired:
-            done = jnp.where(prow == s, per_block + per_block // 2, done)
+            done = jnp.where(prow == s, per_block + per_block // 3, done)
         produce_first(done, live(0) * per_block)
 
     @pl.when(both(pcol > 0, jnp.logical_not(later)))

time: 74.4 us -> 74.5 us (level)
  no operation moved by 1% of the time
where the time goes in v7:
time: 74.5 us; the launch traced here: 74.4 us
  Pallas kernels  73.4 us (99%)
  local copies, waits for them, and re-layouts  1.02 us (1%)
    pallas_call x1, Pallas kernels, on_device(): pl.pallas_call(functools.partial(factor_kernel, prow_count, pcol_count, s...  73.4 us

profile of v7, /device:TPU:26, one launch (start us, length us, event | category | flops | bytes accessed | tf_op | source)
XLA Modules:
  0.0 74.4 jit_solution(17827606309127198468)
XLA Ops:
  0.0 73.4 %shard_map.46 = f32[768,384]{1,0:T(8,128)S(1)} custom-call(f32[768,384]{1,0:T(8,128)} %bitcast.3, s32[3,384]{1,0:T(4,128)} %pivots_ref.1, f32[3,384,384]{2,1,0:T(8,128)} %lower_ref.1, f32[3,384,384]{2,1,0:T(8,128)} %upper_ref.1), custom_call_target="tpu_custom_call" | custom-call | tf_op jit(solution)/shard_map/pallas_call | solution.py:849
  73.4 1.0 %copy.6 = f32[1,1,768,384]{3,2,1,0:T(8,128)} copy(f32[1,1,768,384]{3,2,1,0:T(8,128)S(1)} %bitcast.2) | data formatting | bytes 2359296
